TPU v7x, 32 devices: a whole 2x2x4 slice. The times are simulated.
32 devices in a mesh: gy: 2 (over core), gx: 16 (over z, y, x).
Axes of the slice: x: 2, y: 2, z: 4, core: 2. Of those that a mesh axis runs over, the one named last changes fastest.
Arguments:
- basis_vectors: float32 [36, 64, 128, 256], P(None, 'gx', 'gy'), may hold values from -30 to 30, as said below
- reaction: float32 [64, 128, 256], P('gx', 'gy'), may hold values from 0.5 to 3
Outputs:
- new_vectors: float32 [4, 64, 128, 256], P(None, 'gx', 'gy')
- hessenberg: float32 [40, 4], replicated
Inputs may be any that keep to these rules, and one draw needn't show every extreme that they name: `basis_vectors`: under the inner product the basis vectors are nearly orthonormal.
All inputs are finite; a program needn't handle non-finite values.
Results may differ from a plain program's by a relative error of at most 0.0003.
Values sent between devices are 32-bit elements; how exact they have to be, the bound alone decides.
A program may use at most 128 MiB of HBM per device.

v0:
```python
import functools

import jax
import jax.numpy as jnp
from jax import lax
from jax.experimental import pallas as pl
from jax.experimental.pallas import tpu as pltpu
from jax.sharding import PartitionSpec as P

STEPS = 4
WIND_SPEEDS = (0.9, 0.6, 0.4)
EPSILON = 1e-06
MESH = pl.DeviceIdType.MESH
BLOCK = 6
LOADS = 6


def roll(values, shift, axis):
    return pltpu.roll(values, shift, axis)


def fold_lanes(values):
    parts = [values[:, s : s + 128] for s in range(0, values.shape[1], 128)]
    return functools.reduce(lambda a, b: a + b, parts)


def kernel(
    keep, planes, rows_y, n_gx, n_gy, g1,
    basis, reaction, w_out, h_out,
    vecs, padded, image, react, gram_rows, proj_rows, slots1, slots2, coef,
    load_sem, last_sem, react_sem, out_sem,
    halo_send, halo_recv, send1, recv1, send2, recv2,
):
    width = basis.shape[2]
    rows = planes * rows_y
    padded_count = proj_rows.shape[1]
    gx = lax.axis_index("gx")
    gy = lax.axis_index("gy")
    n1 = n_gy * g1
    n2 = n_gx // g1
    low = lax.rem(gx, g1)
    high = gx // g1
    me1 = gy * g1 + low
    me2 = high
    cells = float(rows * width * n_gx * n_gy)

    last_copies = [
        pltpu.make_async_copy(
            basis.at[keep - 1, p * rows_y : (p + 1) * rows_y],
            padded.at[0, p + 2, 8 : rows_y + 8],
            last_sem.at[p],
        )
        for p in range(planes)
    ]
    for copy in last_copies:
        copy.start()
    bounds = [(g * keep // LOADS, (g + 1) * keep // LOADS) for g in range(LOADS)]
    loads = [
        pltpu.make_async_copy(basis.at[a:b], vecs.at[a:b], load_sem.at[g])
        for g, (a, b) in enumerate(bounds)
    ]
    for copy in loads:
        copy.start()
    react_copy = pltpu.make_async_copy(reaction, react, react_sem)
    react_copy.start()

    has_xl, has_xh = gx > 0, gx < n_gx - 1
    has_yl, has_yh = gy > 0, gy < n_gy - 1

    def member1(d):
        p = lax.rem(me1 + d, n1)
        return p, {"gx": high * g1 + lax.rem(p, g1), "gy": p // g1}

    def member2(d):
        p = lax.rem(me2 + d, n2)
        return p, {"gx": p * g1 + low, "gy": gy}

    barrier = pltpu.get_barrier_semaphore()
    for d in range(1, n1):
        pl.semaphore_signal(barrier, inc=1, device_id=member1(d)[1], device_id_type=MESH)
    for d in range(1, n2):
        pl.semaphore_signal(barrier, inc=1, device_id=member2(d)[1], device_id_type=MESH)
    sides = (
        (has_xh, {"gx": gx + 1, "gy": gy}),
        (has_xl, {"gx": gx - 1, "gy": gy}),
        (has_yh, {"gx": gx, "gy": gy + 1}),
        (has_yl, {"gx": gx, "gy": gy - 1}),
    )
    expected = n1 - 1 + n2 - 1
    for there, device in sides:
        @pl.when(there)
        def _(device=device):
            pl.semaphore_signal(barrier, inc=1, device_id=device, device_id_type=MESH)

        expected = expected + there.astype(jnp.int32)

    zero_plane = jnp.zeros((1, rows_y, width), jnp.float32)
    zero_rows = jnp.zeros((planes, 8, width), jnp.float32)
    for step in range(STEPS):
        @pl.when(jnp.logical_not(has_xl))
        def _(step=step):
            padded[step, 0:1, 8 : rows_y + 8] = zero_plane
            padded[step, 1:2, 8 : rows_y + 8] = zero_plane

        @pl.when(jnp.logical_not(has_xh))
        def _(step=step):
            padded[step, planes + 2 : planes + 3, 8 : rows_y + 8] = zero_plane

        @pl.when(jnp.logical_not(has_yl))
        def _(step=step):
            padded[step, 2 : planes + 2, 0:8] = zero_rows

        @pl.when(jnp.logical_not(has_yh))
        def _(step=step):
            padded[step, 2 : planes + 2, rows_y + 8 : rows_y + 16] = zero_rows

    gram_rows[...] = jnp.zeros(gram_rows.shape, jnp.float32)
    proj_rows[...] = jnp.zeros(proj_rows.shape, jnp.float32)
    pl.semaphore_wait(barrier, expected)

    def halo_copies(step):
        own = pl.ds(2, planes)
        refs = (
            (padded.at[step, planes : planes + 2, 8 : rows_y + 8], padded.at[step, 0:2, 8 : rows_y + 8]),
            (padded.at[step, 2:3, 8 : rows_y + 8], padded.at[step, planes + 2 : planes + 3, 8 : rows_y + 8]),
            (padded.at[step, own, rows_y : rows_y + 8], padded.at[step, own, 0:8]),
            (padded.at[step, own, 8:16], padded.at[step, own, rows_y + 8 : rows_y + 16]),
        )
        return [
            pltpu.make_async_remote_copy(
                src_ref=src, dst_ref=dst,
                send_sem=halo_send.at[step, n], recv_sem=halo_recv.at[step, n],
                device_id=sides[n][1], device_id_type=MESH,
            )
            for n, (src, dst) in enumerate(refs)
        ]

    def start_halo(step, which):
        copies = halo_copies(step)
        for n in which:
            copy = copies[n]

            @pl.when(sides[n][0])
            def _(copy=copy):
                copy.start()

    def wait_halo(step, which):
        copies = halo_copies(step)
        arrives = (has_xl, has_xh, has_yl, has_yh)
        for n in which:
            copy = copies[n]

            @pl.when(arrives[n])
            def _(copy=copy):
                copy.wait_recv()

            @pl.when(sides[n][0])
            def _(copy=copy):
                copy.wait_send()

    stage1 = (slots1, me1, n1, member1, send1, recv1)
    stage2 = (slots2, me2, n2, member2, send2, recv2)

    def exchange(rnd, stage, start, stop, begin):
        slots, me, count, member, send, recv = stage

        def copy_of(slot, d):
            return pltpu.make_async_remote_copy(
                src_ref=slots.at[rnd, slot, start:stop], dst_ref=slots.at[rnd, slot, start:stop],
                send_sem=send.at[rnd, d - 1], recv_sem=recv.at[rnd, slot],
                device_id=member(d)[1], device_id_type=MESH,
            )

        if begin:
            for d in range(1, count):
                copy_of(me, d).start()
            return None
        for d in range(1, count):
            copy_of(member(d)[0], d).wait_recv()
        for d in range(1, count):
            copy_of(me, d).wait_send()
        total = slots[rnd, 0, start:stop]
        for slot in range(1, count):
            total = total + slots[rnd, slot, start:stop]
        return total

    def begin1(rnd, start, stop):
        exchange(rnd, stage1, start, stop, True)

    def begin2(rnd, start, stop):
        slots2[rnd, me2, start:stop] = exchange(rnd, stage1, start, stop, False)
        exchange(rnd, stage2, start, stop, True)

    def finish(rnd, start, stop):
        return exchange(rnd, stage2, start, stop, False) / cells

    def all_sum(rnd, start, stop):
        begin1(rnd, start, stop)
        begin2(rnd, start, stop)
        return finish(rnd, start, stop)

    shape = (padded_count, 128)
    lane = lax.broadcasted_iota(jnp.int32, shape, 1)
    sub = lax.broadcasted_iota(jnp.int32, shape, 0)
    eye = lane == sub
    sub8 = lax.broadcasted_iota(jnp.int32, (8, 128), 0)

    def lane_sum(values):
        return jnp.broadcast_to(jnp.sum(values, axis=1, keepdims=True), values.shape)

    def to_column(row):
        return lane_sum(jnp.where(eye, jnp.broadcast_to(row, shape), 0.0))

    def to_row(column):
        return jnp.sum(jnp.where(eye, column, 0.0), axis=0, keepdims=True)

    def project(load, count, kind):
        for first in range(0, count, 20):
            group = range(first, min(first + 20, count))

            def step(r, sums):
                at = pl.ds(pl.multiple_of(r * 8, 8), 8)
                other = load(at)
                return tuple(
                    acc + fold_lanes(vecs[i, at, :] * other) for i, acc in zip(group, sums)
                )

            zero = jnp.zeros((8, 128), jnp.float32)
            sums = lax.fori_loop(0, rows // 8, step, (zero,) * len(group), unroll=4)
            for i, acc in zip(group, sums):
                proj_rows[kind, i : i + 1, :] = jnp.sum(acc, axis=0, keepdims=True)

    def stencil(step):
        tall = 16
        lanes = lax.broadcasted_iota(jnp.int32, (tall, width), 1)
        sx, sy, sz = WIND_SPEEDS
        centre = 6.0 + 1.5 * (sx + sy + sz)

        def piece(p, q):
            base = pl.multiple_of(q * tall, 8)
            at = pl.ds(pl.multiple_of(base + 8, 8), tall)
            block = padded[step, p + 2, pl.ds(base, tall + 16), :]
            here = block[8 : tall + 8]
            out_at = pl.ds(pl.multiple_of(p * rows_y + base, 8), tall)
            total = -(react[out_at, :] + centre) * here
            total = total + padded[step, p + 3, at, :]
            total = total + (1.0 + 2.0 * sx) * padded[step, p + 1, at, :]
            total = total - (0.5 * sx) * padded[step, p, at, :]
            total = total + roll(block, tall + 15, 0)[8 : tall + 8]
            total = total + (1.0 + 2.0 * sy) * roll(block, 1, 0)[8 : tall + 8]
            total = total - (0.5 * sy) * roll(block, 2, 0)[8 : tall + 8]
            total = total + jnp.where(lanes < width - 1, roll(here, width - 1, 1), 0.0)
            total = total + (1.0 + 2.0 * sz) * jnp.where(lanes >= 1, roll(here, 1, 1), 0.0)
            total = total - (0.5 * sz) * jnp.where(lanes >= 2, roll(here, 2, 1), 0.0)
            image[out_at, :] = total

        inner = range(2, planes - 1)
        wait_halo(step, (2, 3))
        for p in inner:
            @pl.loop(0, rows_y // tall, unroll=True)
            def _(q, p=p):
                piece(p, q)

        wait_halo(step, (0, 1))
        for p in [p for p in range(planes) if p not in inner]:
            @pl.loop(0, rows_y // tall, unroll=True)
            def _(q, p=p):
                piece(p, q)

    def combine(step, count, scale):
        tall = 32 if rows_y % 32 == 0 else 16
        scale_row = jnp.concatenate([scale] * (width // 128), axis=1)

        def plane(p):
            @pl.loop(0, rows_y // tall)
            def _(q):
                at = pl.ds(pl.multiple_of(p * rows_y + q * tall, 8), tall)
                total = image[at, :] * scale_row
                for i in range(count):
                    total = total - coef[i : i + 1, :] * vecs[i, at, :]
                vecs[keep + step, at, :] = total
                if step < STEPS - 1:
                    padded[step + 1, p + 2, pl.ds(pl.multiple_of(q * tall + 8, 8), tall), :] = total

        more = step < STEPS - 1
        done = []
        for part, side in (((planes - 2, planes - 1), 0), ((0,), 1), (range(planes), 2)):
            for p in part:
                if p not in done:
                    plane(p)
                    done.append(p)
            if more:
                start_halo(step + 1, (side,) if side < 2 else (2, 3))

    def send_row(rnd, a_row, b_row):
        slots1[rnd, me1, padded_count : padded_count + 8] = jnp.where(
            sub8 == 0, a_row, jnp.where(sub8 == 1, b_row, 0.0)
        )

    for copy in last_copies:
        copy.wait()
    start_halo(0, (0, 1, 2, 3))
    ready = 0
    blocks = [(s, min(s + BLOCK, keep)) for s in range(0, keep, BLOCK)]
    for jb in range(len(blocks)):
        while ready < LOADS and bounds[ready][0] < blocks[jb][1]:
            loads[ready].wait()
            ready += 1
        for ib in range(jb + 1):
            pairs = [
                (i, j)
                for i in range(*blocks[ib])
                for j in range(*blocks[jb])
                if i <= j
            ]

            def step(r, sums, ib=ib, jb=jb, pairs=pairs):
                at = pl.ds(pl.multiple_of(r * 8, 8), 8)
                for s in range(0, width, 128):
                    needed = sorted(set(range(*blocks[ib])) | set(range(*blocks[jb])))
                    held = {i: vecs[i, at, s : s + 128] for i in needed}
                    sums = tuple(acc + held[i] * held[j] for (i, j), acc in zip(pairs, sums))
                return sums

            zero = jnp.zeros((8, 128), jnp.float32)
            sums = lax.fori_loop(0, rows // 8, step, (zero,) * len(pairs))
            for (i, j), acc in zip(pairs, sums):
                line = jnp.sum(acc, axis=0, keepdims=True)
                gram_rows[i, j : j + 1, :] = line
                if i != j:
                    gram_rows[j, i : i + 1, :] = line
    local_gram = jnp.zeros(shape, jnp.float32)
    for i in range(keep):
        local_gram = jnp.where(lane == i, lane_sum(gram_rows[i]), local_gram)
    slots1[STEPS + 1, me1, 0:padded_count] = local_gram
    react_copy.wait()
    begin1(STEPS + 1, 0, padded_count)

    gram = None
    scales = jnp.ones(shape, jnp.float32)
    hess = jnp.zeros(shape, jnp.float32)
    b_row = jnp.zeros((1, 128), jnp.float32)
    out_copies = []
    for step in range(STEPS):
        count = keep + step
        last = count - 1
        if step > 0:
            project(lambda at: vecs[last, at, :], count, 1)
            b_row = to_row(lane_sum(proj_rows[1]))
        stencil(step)
        project(lambda at: image[at, :], count, 0)
        send_row(step, to_row(lane_sum(proj_rows[0])), b_row)
        if step == 0:
            begin1(0, padded_count, padded_count + 8)
            begin2(STEPS + 1, 0, padded_count)
            begin2(0, padded_count, padded_count + 8)
            gram = finish(STEPS + 1, 0, padded_count)
            total = finish(0, padded_count, padded_count + 8)
            scale = jnp.ones((1, 128), jnp.float32)
        else:
            total = all_sum(step, padded_count, padded_count + 8)
            overlap = to_column(total[1:2])
            norm = jnp.sqrt(overlap[last : last + 1] + EPSILON)
            scale = 1.0 / norm
            hess = jnp.where((lane == step - 1) & (sub == last), norm, hess)
            scales = jnp.where(sub == last, scale, scales)
            column = jnp.where(sub < count, overlap * scales * scale, 0.0)
            gram = jnp.where(sub == last, to_row(column), gram)
            gram = jnp.where(lane == last, column, gram)
        first = jnp.where(sub < count, to_column(total[0:1]) * scales * scale, 0.0)
        weights = first + (first - lane_sum(gram * to_row(first)))
        weights = jnp.where(sub < count, weights, 0.0)
        hess = jnp.where((lane == step) & (sub < count), weights, hess)
        scaled = weights * scales
        coef[...] = jnp.concatenate([scaled] * (width // 128), axis=1)
        combine(step, count, scale)
        copy = pltpu.make_async_copy(vecs.at[keep + step], w_out.at[step], out_sem.at[step])
        copy.start()
        out_copies.append(copy)

    last = keep + STEPS - 1

    def square(r, acc):
        values = vecs[last, pl.ds(pl.multiple_of(r * 8, 8), 8), :]
        return acc + fold_lanes(values * values)

    acc = lax.fori_loop(0, rows // 8, square, jnp.zeros((8, 128), jnp.float32))
    line = lane_sum(jnp.sum(acc, axis=0, keepdims=True))
    send_row(STEPS, line, line)
    total = all_sum(STEPS, padded_count, padded_count + 8)
    norm = jnp.sqrt(total[0:1] + EPSILON)
    hess = jnp.where((lane == STEPS - 1) & (sub == last), norm, hess)
    h_out[...] = hess
    for copy in out_copies:
        copy.wait()


def group_of(count):
    for size in (4, 2):
        if count % size == 0:
            return size
    return 1


def body(basis_vectors, reaction):
    keep, planes, rows_y, width = basis_vectors.shape
    n_gx, n_gy = lax.axis_size("gx"), lax.axis_size("gy")
    g1 = group_of(n_gx)
    n1, n2 = g1 * n_gy, n_gx // g1
    size = keep + STEPS
    padded_count = -(-size // 8) * 8
    rows = planes * rows_y
    rounds = STEPS + 2
    f32 = jnp.float32
    dma = pltpu.SemaphoreType.DMA
    w, h = pl.pallas_call(
        functools.partial(kernel, keep, planes, rows_y, n_gx, n_gy, g1),
        out_shape=(
            jax.ShapeDtypeStruct((STEPS, rows, width), f32),
            jax.ShapeDtypeStruct((padded_count, 128), f32),
        ),
        in_specs=[pl.BlockSpec(memory_space=pl.ANY)] * 2,
        out_specs=(
            pl.BlockSpec(memory_space=pl.ANY),
            pl.BlockSpec(memory_space=pltpu.VMEM),
        ),
        scratch_shapes=[
            pltpu.VMEM((size, rows, width), f32),
            pltpu.VMEM((STEPS, planes + 3, rows_y + 16, width), f32),
            pltpu.VMEM((rows, width), f32),
            pltpu.VMEM((rows, width), f32),
            pltpu.VMEM((keep, padded_count, 128), f32),
            pltpu.VMEM((2, padded_count, 128), f32),
            pltpu.VMEM((rounds, n1, padded_count + 8, 128), f32),
            pltpu.VMEM((rounds, n2, padded_count + 8, 128), f32),
            pltpu.VMEM((padded_count, width), f32),
            dma((LOADS,)),
            dma((planes,)),
            dma,
            dma((STEPS,)),
            dma((STEPS, 4)),
            dma((STEPS, 4)),
            dma((rounds, n1)),
            dma((rounds, n1)),
            dma((rounds, n2)),
            dma((rounds, n2)),
        ],
        compiler_params=pltpu.CompilerParams(
            collective_id=0, has_side_effects=True, vmem_limit_bytes=48 * 1024 * 1024
        ),
    )(basis_vectors.reshape(keep, rows, width), reaction.reshape(rows, width))
    norms = jnp.stack([h[keep + j, j] for j in range(STEPS)])
    vectors = w / norms[:, None, None]
    return vectors.reshape(STEPS, planes, rows_y, width), h[:size, :STEPS]


def solution(mesh):
    in_specs = (P(None, "gx", "gy", None), P("gx", "gy", None))
    out_specs = (P(None, "gx", "gy", None), P())
    return jax.shard_map(body, mesh=mesh, in_specs=in_specs, out_specs=out_specs, check_vma=False)
```

profile of v0, /device:TPU:0, one launch (start us, length us, event | category | flops | bytes accessed | tf_op | source)
XLA Modules:
  0.0 93.2 jit_solution(2845265465172320896)
XLA Ops:
  0.6 0.0 copy-start
  0.6 0.9 %copy-done = f32[4,64,256]{2,1,0:T(8,128)S(1)} copy-done((f32[4,64,256]{2,1,0:T(8,128)S(1)}, f32[4,64,256]{2,1,0:T(8,128)}, u32[]{:S(2)}) %copy-start) | copy-done | bytes 262168
  1.6 86.6 %shard_map.41 = (f32[4,256,256]{2,1,0:T(8,128)S(1)}, f32[40,128]{1,0:T(8,128)S(1)}) custom-call(f32[36,256,256]{2,1,0:T(8,128)} %bitcast.10, f32[256,256]{1,0:T(8,128)S(1)} %bitcast.8), custom_call_target="tpu_custom_call" | custom-call | tf_op jit(solution)/shard_map/pallas_call | solution.py:416
  88.2 0.7 copy.4
  88.9 0.6 fusion
  89.5 2.6 %pad_maximum_fusion = f32[4]{0:T(128)S(1)} fusion(f32[1]{0:T(128)} %bitcast.5, f32[1]{0:T(128)} %bitcast.4, f32[1]{0:T(128)} %bitcast.3, f32[1]{0:T(128)} %bitcast.2), kind=kLoop, calls=%fused_computation.1 | loop fusion | flops 12 | bytes 32 | tf_op jit(solution)/shard_map/stack | solution.py:452
  92.1 1.1 %broadcast_divide_fusion = f32[4,256,256]{2,1,0:T(8,128)} fusion(f32[4,256,256]{2,1,0:T(8,128)S(1)} %get-tuple-element.4, f32[4]{0:T(128)S(1)} %pad_maximum_fusion), kind=kLoop, calls=%fused_computation | loop fusion | flops 262144 | bytes 2097168 | tf_op jit(solution)/shard_map/div | solution.py:453
Async XLA Ops:
  0.6 1.0 %copy-start = (f32[4,64,256]{2,1,0:T(8,128)S(1)}, f32[4,64,256]{2,1,0:T(8,128)}, u32[]{:S(2)}) copy-start(f32[4,64,256]{2,1,0:T(8,128)} %param.3) | copy-start | bytes 786436
where the time goes:
time: 93.4 us; the launch traced here: 93.2 us
  Pallas kernels  86.6 us (93%)
  other arithmetic  3.72 us (4%)
  local copies, waits for them, and re-layouts  2.24 us (2%)
    pallas_call x1, Pallas kernels, body(): pl.pallas_call(functools.partial(kernel, keep, planes, rows_y, n_gx, n_gy...  86.6 us
    another operation x1, other arithmetic, body(): norms = jnp.stack([h[keep + j, j] for j in range(STEPS)])  2.58 us

commit v1 on v0

v1 whole, which is shorter than its diff:
```python
import functools

import jax
import jax.numpy as jnp
from jax import lax
from jax.experimental import pallas as pl
from jax.experimental.pallas import tpu as pltpu
from jax.sharding import PartitionSpec as P

STEPS = 4
WIND_SPEEDS = (0.9, 0.6, 0.4)
EPSILON = 1e-06
MESH = pl.DeviceIdType.MESH
CHUNK = 16


def roll(values, shift, axis):
    return pltpu.roll(values, shift, axis)


def fold_lanes(values):
    parts = [values[:, s : s + 128] for s in range(0, values.shape[1], 128)]
    return functools.reduce(lambda a, b: a + b, parts)


def tree(parts):
    while len(parts) > 1:
        parts = [
            parts[i] + parts[i + 1] if i + 1 < len(parts) else parts[i]
            for i in range(0, len(parts), 2)
        ]
    return parts[0]


def kernel(
    keep, planes, rows_y, n_gx, n_gy, g1,
    basis, reaction, w_out, h_out,
    vecs, padded, image, react, head, tail, squares, proj, slots1, slots2, slots, coef,
    load_sem, last_sem, react_sem,
    halo_send, halo_recv, send1, recv1, send2, recv2, sends, recvs, ready,
):
    width = basis.shape[2]
    rows = planes * rows_y
    padded_count = proj.shape[1]
    gx = lax.axis_index("gx")
    gy = lax.axis_index("gy")
    n1 = n_gy * g1
    n2 = n_gx // g1
    low = lax.rem(gx, g1)
    high = gx // g1
    me1 = gy * g1 + low
    me2 = high
    cells = float(rows * width * n_gx * n_gy)

    last_copies = [
        pltpu.make_async_copy(
            basis.at[keep - 1, p * rows_y : (p + 1) * rows_y],
            padded.at[0, p + 2, 8 : rows_y + 8],
            last_sem.at[p],
        )
        for p in range(planes)
    ]
    for copy in last_copies:
        copy.start()
    chunks = rows // CHUNK

    def load(c):
        at = pl.ds(pl.multiple_of(c * CHUNK, CHUNK), CHUNK)
        return pltpu.make_async_copy(basis.at[:, at], vecs.at[0:keep, at], load_sem.at[c])

    @pl.loop(0, chunks)
    def _(c):
        load(c).start()

    react_copy = pltpu.make_async_copy(reaction, react, react_sem)
    react_copy.start()

    has_xl, has_xh = gx > 0, gx < n_gx - 1
    has_yl, has_yh = gy > 0, gy < n_gy - 1

    def member1(d):
        p = lax.rem(me1 + d, n1)
        return p, {"gx": high * g1 + lax.rem(p, g1), "gy": p // g1}

    def member2(d):
        p = lax.rem(me2 + d, n2)
        return p, {"gx": p * g1 + low, "gy": gy}

    me = gx * n_gy + gy
    devices = n_gx * n_gy

    def member(d):
        p = lax.rem(me + d, devices)
        return {"gx": p // n_gy, "gy": lax.rem(p, n_gy)}

    barrier = pltpu.get_barrier_semaphore()
    for d in range(1, n1):
        pl.semaphore_signal(barrier, inc=1, device_id=member1(d)[1], device_id_type=MESH)
    for d in range(1, n2):
        pl.semaphore_signal(barrier, inc=1, device_id=member2(d)[1], device_id_type=MESH)
    sides = (
        (has_xh, {"gx": gx + 1, "gy": gy}),
        (has_xl, {"gx": gx - 1, "gy": gy}),
        (has_yh, {"gx": gx, "gy": gy + 1}),
        (has_yl, {"gx": gx, "gy": gy - 1}),
    )
    expected = n1 - 1 + n2 - 1
    for there, device in sides:
        @pl.when(there)
        def _(device=device):
            pl.semaphore_signal(barrier, inc=1, device_id=device, device_id_type=MESH)

        expected = expected + there.astype(jnp.int32)

    zero_plane = jnp.zeros((1, rows_y, width), jnp.float32)
    zero_rows = jnp.zeros((planes, 8, width), jnp.float32)
    for step in range(STEPS):
        @pl.when(jnp.logical_not(has_xl))
        def _(step=step):
            padded[step, 0:1, 8 : rows_y + 8] = zero_plane
            padded[step, 1:2, 8 : rows_y + 8] = zero_plane

        @pl.when(jnp.logical_not(has_xh))
        def _(step=step):
            padded[step, planes + 2 : planes + 3, 8 : rows_y + 8] = zero_plane

        @pl.when(jnp.logical_not(has_yl))
        def _(step=step):
            padded[step, 2 : planes + 2, 0:8] = zero_rows

        @pl.when(jnp.logical_not(has_yh))
        def _(step=step):
            padded[step, 2 : planes + 2, rows_y + 8 : rows_y + 16] = zero_rows

    head[...] = jnp.zeros(head.shape, jnp.float32)
    tail[...] = jnp.zeros(tail.shape, jnp.float32)
    squares[...] = jnp.zeros(squares.shape, jnp.float32)
    proj[...] = jnp.zeros(proj.shape, jnp.float32)
    pl.semaphore_wait(barrier, expected)
    for d in range(1, n2):
        pl.semaphore_signal(ready, inc=1, device_id=member2(d)[1], device_id_type=MESH)

    def halo_copies(step):
        own = pl.ds(2, planes)
        refs = (
            (padded.at[step, planes : planes + 2, 8 : rows_y + 8], padded.at[step, 0:2, 8 : rows_y + 8]),
            (padded.at[step, 2:3, 8 : rows_y + 8], padded.at[step, planes + 2 : planes + 3, 8 : rows_y + 8]),
            (padded.at[step, own, rows_y : rows_y + 8], padded.at[step, own, 0:8]),
            (padded.at[step, own, 8:16], padded.at[step, own, rows_y + 8 : rows_y + 16]),
        )
        return [
            pltpu.make_async_remote_copy(
                src_ref=src, dst_ref=dst,
                send_sem=halo_send.at[step, n], recv_sem=halo_recv.at[step, n],
                device_id=sides[n][1], device_id_type=MESH,
            )
            for n, (src, dst) in enumerate(refs)
        ]

    def start_halo(step, which):
        copies = halo_copies(step)
        for n in which:
            copy = copies[n]

            @pl.when(sides[n][0])
            def _(copy=copy):
                copy.start()

    def wait_halo(step, which):
        copies = halo_copies(step)
        arrives = (has_xl, has_xh, has_yl, has_yh)
        for n in which:
            copy = copies[n]

            @pl.when(arrives[n])
            def _(copy=copy):
                copy.wait_recv()

            @pl.when(sides[n][0])
            def _(copy=copy):
                copy.wait_send()

    stage1 = (slots1, me1, n1, member1, send1, recv1)
    stage2 = (slots2, me2, n2, member2, send2, recv2)

    def exchange(stage, begin):
        slots, me, count, member, send, recv = stage

        def copy_of(slot, d):
            return pltpu.make_async_remote_copy(
                src_ref=slots.at[slot], dst_ref=slots.at[slot],
                send_sem=send.at[d - 1], recv_sem=recv.at[slot],
                device_id=member(d)[1], device_id_type=MESH,
            )

        if begin:
            for d in range(1, count):
                copy_of(me, d).start()
            return None
        for d in range(1, count):
            copy_of(member(d)[0], d).wait_recv()
        for d in range(1, count):
            copy_of(me, d).wait_send()
        return tree([slots[slot] for slot in range(count)])

    def begin_sum(rnd, row):
        slots[rnd, me] = row
        for d in range(1, devices):
            pltpu.make_async_remote_copy(
                src_ref=slots.at[rnd, me], dst_ref=slots.at[rnd, me],
                send_sem=sends.at[rnd], recv_sem=recvs.at[rnd],
                device_id=member(d), device_id_type=MESH,
            ).start()

    def finish_sum(rnd):
        every = pltpu.make_async_remote_copy(
            src_ref=slots.at[rnd, 0 : devices - 1], dst_ref=slots.at[rnd, 0 : devices - 1],
            send_sem=sends.at[rnd], recv_sem=recvs.at[rnd],
            device_id=member(1), device_id_type=MESH,
        )
        every.wait_recv()
        every.wait_send()
        return tree([slots[rnd, slot] for slot in range(devices)]) / cells

    shape = (padded_count, 128)
    lane = lax.broadcasted_iota(jnp.int32, shape, 1)
    sub = lax.broadcasted_iota(jnp.int32, shape, 0)
    eye = lane == sub
    eye_high = lane == sub + 64
    lane8 = lax.broadcasted_iota(jnp.int32, (8, 128), 1)
    sub8 = lax.broadcasted_iota(jnp.int32, (8, 128), 0)

    def lane_sum(values):
        return jnp.broadcast_to(jnp.sum(values, axis=1, keepdims=True), values.shape)

    def to_column(row, where=eye):
        return lane_sum(jnp.where(where, jnp.broadcast_to(row, shape), 0.0))

    def to_row(column, where=eye):
        return jnp.sum(jnp.where(where, column, 0.0), axis=0, keepdims=True)

    def project(read, count, kind, spans, fresh):
        for first in range(0, count, 20):
            group = range(first, min(first + 20, count))

            def step(r, sums):
                at = pl.ds(pl.multiple_of(r * 8, 8), 8)
                other = read(at)
                return tuple(
                    acc + fold_lanes(vecs[i, at, :] * other) for i, acc in zip(group, sums)
                )

            if fresh:
                sums = (jnp.zeros((8, 128), jnp.float32),) * len(group)
            else:
                sums = tuple(proj[kind, i] for i in group)
            for start, stop in spans:
                sums = lax.fori_loop(start // 8, stop // 8, step, sums, unroll=4)
            for i, acc in zip(group, sums):
                proj[kind, i] = acc

    def projected(kind):
        return lane_sum(jnp.sum(proj[kind], axis=1))

    def stencil(step, part):
        tall = 16
        lanes = lax.broadcasted_iota(jnp.int32, (tall, width), 1)
        sx, sy, sz = WIND_SPEEDS
        centre = 6.0 + 1.5 * (sx + sy + sz)

        def piece(p, q):
            base = pl.multiple_of(q * tall, 8)
            at = pl.ds(pl.multiple_of(base + 8, 8), tall)
            block = padded[step, p + 2, pl.ds(base, tall + 16), :]
            here = block[8 : tall + 8]
            out_at = pl.ds(pl.multiple_of(p * rows_y + base, 8), tall)
            total = -(react[out_at, :] + centre) * here
            total = total + padded[step, p + 3, at, :]
            total = total + (1.0 + 2.0 * sx) * padded[step, p + 1, at, :]
            total = total - (0.5 * sx) * padded[step, p, at, :]
            total = total + roll(block, tall + 15, 0)[8 : tall + 8]
            total = total + (1.0 + 2.0 * sy) * roll(block, 1, 0)[8 : tall + 8]
            total = total - (0.5 * sy) * roll(block, 2, 0)[8 : tall + 8]
            total = total + jnp.where(lanes < width - 1, roll(here, width - 1, 1), 0.0)
            total = total + (1.0 + 2.0 * sz) * jnp.where(lanes >= 1, roll(here, 1, 1), 0.0)
            total = total - (0.5 * sz) * jnp.where(lanes >= 2, roll(here, 2, 1), 0.0)
            image[out_at, :] = total

        for p in part:
            @pl.loop(0, rows_y // tall, unroll=True)
            def _(q, p=p):
                piece(p, q)

    def combine(step, count, scale):
        tall = 32 if rows_y % 32 == 0 else 16
        scale_row = jnp.concatenate([scale] * (width // 128), axis=1)

        def plane(p):
            @pl.loop(0, rows_y // tall)
            def _(q):
                at = pl.ds(pl.multiple_of(p * rows_y + q * tall, 8), tall)
                total = image[at, :] * scale_row
                for i in range(count):
                    total = total - coef[i : i + 1, :] * vecs[i, at, :]
                vecs[keep + step, at, :] = total
                if step < STEPS - 1:
                    padded[step + 1, p + 2, pl.ds(pl.multiple_of(q * tall + 8, 8), tall), :] = total

        more = step < STEPS - 1
        done = []
        for part, side in (((planes - 2, planes - 1), 0), ((0,), 1), (range(planes), 2)):
            for p in part:
                if p not in done:
                    plane(p)
                    done.append(p)
            if more:
                start_halo(step + 1, (side,) if side < 2 else (2, 3))

    def split(values):
        scaled = values * 65537.0
        high = scaled - (scaled - values)
        return high, values - high

    def outer(a, b):
        return lax.dot_general(
            a, b, (((1,), (1,)), ((), ())), preferred_element_type=jnp.float32
        )

    cut = head.shape[1]
    late = keep * 8 - 128

    def gram_block(r):
        at = pl.ds(pl.multiple_of(r, 8), 8)
        values = vecs[0:keep, at, :].reshape(keep * 8, width)
        power = values * values
        squares[...] = squares[...] + power[:, :128] + power[:, 128:]
        high, low = split(values)
        left = jnp.concatenate([high[:cut] * 0.5, high[cut:]], axis=0)
        first = outer(left, high[:cut]) + outer(low, high[:cut])
        second = outer(low, high[late:])
        third = outer(high[cut:] * 0.5, high[late:])
        return first, second, third

    for copy in last_copies:
        copy.wait()
    start_halo(0, (0, 1, 2, 3))

    @pl.loop(0, chunks)
    def _(c):
        load(c).wait()
        found = [gram_block(c * CHUNK + s) for s in range(0, CHUNK, 8)]
        first, second, third = (functools.reduce(lambda a, b: a + b, f) for f in zip(*found))
        head[...] = head[...] + first
        tail[...] = tail[...] + second
        tail[cut:, :] = tail[cut:, :] + third

    def picked(values, start):
        row = lax.broadcasted_iota(jnp.int32, values.shape, 0)
        column = lax.broadcasted_iota(jnp.int32, values.shape, 1)
        use = (lax.rem(row, 8) == lax.rem(column, 8)) & (column + start >= (cut if start else 0))
        kept = jnp.where(use, values, 0.0)
        return jnp.sum(kept.reshape(keep, 8, values.shape[1]), axis=1)

    spread = jnp.concatenate([picked(head[...], 0), picked(tail[...], late)], axis=1)
    place = lax.broadcasted_iota(jnp.int32, (cut + 128, 128), 0)
    place = jnp.where(place < cut, place, place - cut + late) // 8
    choose = (place == lax.broadcasted_iota(jnp.int32, place.shape, 1)).astype(jnp.float32)
    exact = lax.Precision.HIGHEST
    half = jnp.dot(spread, choose, precision=exact, preferred_element_type=jnp.float32)
    turned = lax.dot_general(
        choose, spread, (((0,), (1,)), ((), ())), precision=exact,
        preferred_element_type=jnp.float32,
    )
    diagonal = jnp.sum(jnp.sum(squares[...].reshape(keep, 8, 128), axis=1), axis=1, keepdims=True)
    lane_k = lax.broadcasted_iota(jnp.int32, (keep, 128), 1)
    sub_k = lax.broadcasted_iota(jnp.int32, (keep, 128), 0)
    image[0:keep, 0:128] = half
    image[0:128, 128:256] = jnp.zeros((128, 128), jnp.float32)
    image[0:128, 128 : 128 + keep] = turned
    both = half + image[0:keep, 128:256]
    local_gram = jnp.where(lane_k == sub_k, diagonal, both)
    slots1[me1] = jnp.zeros(slots1.shape[1:], jnp.float32)
    slots1[me1, 0:keep] = local_gram
    react_copy.wait()
    exchange(stage1, True)

    everything = [(0, rows)]
    inner = range(2, planes - 1)
    edge = [p for p in range(planes) if p not in inner]
    inner_spans = [(p * rows_y, (p + 1) * rows_y) for p in inner]
    edge_spans = [(p * rows_y, (p + 1) * rows_y) for p in edge]

    def emit(step, scale):
        scale_row = jnp.concatenate([scale] * (width // 128), axis=1)

        @pl.loop(0, rows // 32)
        def _(q):
            at = pl.ds(pl.multiple_of(q * 32, 32), 32)
            w_out[step, at, :] = vecs[keep + step, at, :] * scale_row

    gram = None
    scales = jnp.ones(shape, jnp.float32)
    hess = jnp.zeros((8, 128), jnp.float32)
    b_row = jnp.zeros((1, 128), jnp.float32)
    scale = jnp.ones((1, 128), jnp.float32)
    for step in range(STEPS):
        count = keep + step
        last = count - 1
        if step > 0:
            project(lambda at: vecs[last, at, :], count, 1, everything, True)
            b_row = to_row(projected(1), eye_high)
        wait_halo(step, (2, 3))
        stencil(step, inner)
        project(lambda at: image[at, :], count, 0, inner_spans, True)
        if step > 1:
            emit(step - 2, scale)
        wait_halo(step, (0, 1))
        stencil(step, edge)
        project(lambda at: image[at, :], count, 0, edge_spans, False)
        row = to_row(projected(0)) + b_row
        if step == 0:
            pl.semaphore_wait(ready, n2 - 1)
        begin_sum(step, row)
        if step == 0:
            slots2[me2] = exchange(stage1, False)
            exchange(stage2, True)
            gram = exchange(stage2, False) / cells
            total = finish_sum(0)
        else:
            total = finish_sum(step)
            overlap = to_column(total, eye_high)
            norm = jnp.sqrt(overlap[last : last + 1] + EPSILON)
            scale = 1.0 / norm
            hess = jnp.where((sub8 == step - 1) & (lane8 == last), norm, hess)
            scales = jnp.where(sub == last, scale, scales)
            column = jnp.where(sub < count, overlap * scales * scale, 0.0)
            gram = jnp.where(sub == last, to_row(column), gram)
            gram = jnp.where(lane == last, column, gram)
        first = jnp.where(sub < count, to_column(total) * scales * scale, 0.0)
        weights = first + (first - lane_sum(gram * to_row(first)))
        weights = jnp.where(sub < count, weights, 0.0)
        scaled = weights * scales
        coef[...] = jnp.concatenate([scaled] * (width // 128), axis=1)
        combine(step, count, scale)
        hess = jnp.where(sub8 == step, to_row(weights), hess)

    last = keep + STEPS - 1

    def square(r, acc):
        values = vecs[last, pl.ds(pl.multiple_of(r * 8, 8), 8), :]
        return acc + fold_lanes(values * values)

    acc = lax.fori_loop(0, rows // 8, square, jnp.zeros((8, 128), jnp.float32), unroll=4)
    begin_sum(STEPS, lane_sum(jnp.sum(acc, axis=0, keepdims=True)))
    emit(STEPS - 2, scale)
    total = finish_sum(STEPS)
    norm = jnp.sqrt(total + EPSILON)
    hess = jnp.where((sub8 == STEPS - 1) & (lane8 == last), norm, hess)
    h_out[...] = hess
    emit(STEPS - 1, 1.0 / norm)


def group_of(count):
    for size in (4, 2):
        if count % size == 0:
            return size
    return 1


def body(basis_vectors, reaction):
    keep, planes, rows_y, width = basis_vectors.shape
    n_gx, n_gy = lax.axis_size("gx"), lax.axis_size("gy")
    g1 = group_of(n_gx)
    n1, n2 = g1 * n_gy, n_gx // g1
    size = keep + STEPS
    padded_count = -(-size // 8) * 8
    rows = planes * rows_y
    rounds = STEPS + 1
    f32 = jnp.float32
    dma = pltpu.SemaphoreType.DMA
    w, h = pl.pallas_call(
        functools.partial(kernel, keep, planes, rows_y, n_gx, n_gy, g1),
        out_shape=(
            jax.ShapeDtypeStruct((STEPS, rows, width), f32),
            jax.ShapeDtypeStruct((8, 128), f32),
        ),
        in_specs=[pl.BlockSpec(memory_space=pltpu.HBM)] * 2,
        out_specs=(pl.BlockSpec(memory_space=pltpu.VMEM),) * 2,
        scratch_shapes=[
            pltpu.VMEM((size, rows, width), f32),
            pltpu.VMEM((STEPS, planes + 3, rows_y + 16, width), f32),
            pltpu.VMEM((rows, width), f32),
            pltpu.VMEM((rows, width), f32),
            pltpu.VMEM((keep * 8, 256), f32),
            pltpu.VMEM((keep * 8, 128), f32),
            pltpu.VMEM((keep * 8, 128), f32),
            pltpu.VMEM((2, padded_count, 8, 128), f32),
            pltpu.VMEM((n1, padded_count, 128), f32),
            pltpu.VMEM((n2, padded_count, 128), f32),
            pltpu.VMEM((rounds, n_gx * n_gy, 1, 128), f32),
            pltpu.VMEM((padded_count, width), f32),
            dma((rows // CHUNK,)),
            dma((planes,)),
            dma,
            dma((STEPS, 4)),
            dma((STEPS, 4)),
            dma((n1,)),
            dma((n1,)),
            dma((n2,)),
            dma((n2,)),
            dma((rounds,)),
            dma((rounds,)),
            pltpu.SemaphoreType.REGULAR,
        ],
        compiler_params=pltpu.CompilerParams(
            collective_id=0, has_side_effects=True, vmem_limit_bytes=48 * 1024 * 1024
        ),
    )(basis_vectors.reshape(keep, rows, width), reaction.reshape(rows, width))
    return w.reshape(STEPS, planes, rows_y, width), h[:STEPS, :size].T


def solution(mesh):
    in_specs = (P(None, "gx", "gy", None), P("gx", "gy", None))
    out_specs = (P(None, "gx", "gy", None), P())
    return jax.shard_map(body, mesh=mesh, in_specs=in_specs, out_specs=out_specs, check_vma=False)
```

time: 93.4 us -> 68.1 us (0.73)
  Pallas kernels: 86.6 us -> 64.8 us
  other arithmetic: 3.72 us -> 0 us
    pallas_call x1, Pallas kernels: 86.6 us -> 64.8 us  [body(): pl.pallas_call(functools.partial(kernel, keep, planes, rows_y, n_gx, n_gy...]
    another operation x1 -> x0, other arithmetic: 2.58 us -> none  [body(): norms = jnp.stack([h[keep + j, j] for j in range(STEPS)])]
    div x1 -> x0, other arithmetic: 1.14 us -> none  [body(): vectors = w / norms[:, None, None]]
where the time goes in v1:
time: 68.1 us; the launch traced here: 67.9 us
  Pallas kernels  64.8 us (95%)
  local copies, waits for them, and re-layouts  2.49 us (4%)
    pallas_call x1, Pallas kernels, body(): pl.pallas_call(functools.partial(kernel, keep, planes, rows_y, n_gx, n_gy...  64.8 us
    unnamed x3, local copies, waits for them, and re-layouts  1.91 us

profile of v1, /device:TPU:0, one launch (start us, length us, event | category | flops | bytes accessed | tf_op | source)
XLA Modules:
  0.0 67.9 jit_solution(12269314711850675850)
XLA Ops:
  0.6 0.0 copy-start
  0.6 0.9 %copy-done = f32[4,64,256]{2,1,0:T(8,128)S(1)} copy-done((f32[4,64,256]{2,1,0:T(8,128)S(1)}, f32[4,64,256]{2,1,0:T(8,128)}, u32[]{:S(2)}) %copy-start) | copy-done | bytes 262168
  1.6 64.8 %shard_map.41 = (f32[4,256,256]{2,1,0:T(8,128)S(1)}, f32[8,128]{1,0:T(8,128)S(1)}) custom-call(f32[36,256,256]{2,1,0:T(8,128)} %bitcast.7, f32[256,256]{1,0:T(8,128)S(1)} %bitcast.6), custom_call_target="tpu_custom_call" | custom-call | tf_op jit(solution)/shard_map/pallas_call | solution.py:481
  66.4 0.6 slice_bitcast_fusion
  66.9 1.0 %copy.5 = f32[4,4,64,256]{3,2,1,0:T(8,128)} copy(f32[4,4,64,256]{3,2,1,0:T(8,128)S(1)} %bitcast.5) | data formatting | bytes 2097152
Async XLA Ops:
  0.6 1.0 %copy-start = (f32[4,64,256]{2,1,0:T(8,128)S(1)}, f32[4,64,256]{2,1,0:T(8,128)}, u32[]{:S(2)}) copy-start(f32[4,64,256]{2,1,0:T(8,128)} %param.3) | copy-start | bytes 786436

commit v2 on v1

--- a/solution.py
+++ b/solution.py
@@ -11,7 +11,7 @@
 WIND_SPEEDS = (0.9, 0.6, 0.4)
 EPSILON = 1e-06
 MESH = pl.DeviceIdType.MESH
-CHUNK = 16
+CHUNK = 32
 
 
 def roll(values, shift, axis):
@@ -35,7 +35,7 @@
 def kernel(
     keep, planes, rows_y, n_gx, n_gy, g1,
     basis, reaction, w_out, h_out,
-    vecs, padded, image, react, head, tail, squares, proj, slots1, slots2, slots, coef,
+    vecs, padded, image, react, head, tail, squares, pack, proj, slots1, slots2, slots, coef,
     load_sem, last_sem, react_sem,
     halo_send, halo_recv, send1, recv1, send2, recv2, sends, recvs, ready,
 ):
@@ -104,6 +104,8 @@
         (has_yh, {"gx": gx, "gy": gy + 1}),
         (has_yl, {"gx": gx, "gy": gy - 1}),
     )
+    even = lax.rem(gx, 2) == 0
+    odd = jnp.logical_not(even)
     expected = n1 - 1 + n2 - 1
     for there, device in sides:
         @pl.when(there)
@@ -136,47 +138,50 @@
     tail[...] = jnp.zeros(tail.shape, jnp.float32)
     squares[...] = jnp.zeros(squares.shape, jnp.float32)
     proj[...] = jnp.zeros(proj.shape, jnp.float32)
-    pl.semaphore_wait(barrier, expected)
-    for d in range(1, n2):
-        pl.semaphore_signal(ready, inc=1, device_id=member2(d)[1], device_id_type=MESH)
-
     def halo_copies(step):
         own = pl.ds(2, planes)
+        inside = slice(8, rows_y + 8)
         refs = (
-            (padded.at[step, planes : planes + 2, 8 : rows_y + 8], padded.at[step, 0:2, 8 : rows_y + 8]),
-            (padded.at[step, 2:3, 8 : rows_y + 8], padded.at[step, planes + 2 : planes + 3, 8 : rows_y + 8]),
-            (padded.at[step, own, rows_y : rows_y + 8], padded.at[step, own, 0:8]),
-            (padded.at[step, own, 8:16], padded.at[step, own, rows_y + 8 : rows_y + 16]),
+            (0, padded.at[step, planes + 1, inside], padded.at[step, 1, inside]),
+            (0, padded.at[step, planes, inside], padded.at[step, 0, inside]),
+            (1, padded.at[step, 2, inside], padded.at[step, planes + 2, inside]),
+            (2, padded.at[step, own, rows_y : rows_y + 8], padded.at[step, own, 0:8]),
+            (3, padded.at[step, own, 8:16], padded.at[step, own, rows_y + 8 : rows_y + 16]),
         )
         return [
-            pltpu.make_async_remote_copy(
-                src_ref=src, dst_ref=dst,
-                send_sem=halo_send.at[step, n], recv_sem=halo_recv.at[step, n],
-                device_id=sides[n][1], device_id_type=MESH,
+            (
+                sides[side][0],
+                (has_xl, has_xh, has_yl, has_yh)[side],
+                pltpu.make_async_remote_copy(
+                    src_ref=src, dst_ref=dst,
+                    send_sem=halo_send.at[step, n], recv_sem=halo_recv.at[step, n],
+                    device_id=sides[side][1], device_id_type=MESH,
+                ),
             )
-            for n, (src, dst) in enumerate(refs)
+            for n, (side, src, dst) in enumerate(refs)
         ]
 
-    def start_halo(step, which):
+    def start_halo(step, which, where=None):
         copies = halo_copies(step)
         for n in which:
-            copy = copies[n]
-
-            @pl.when(sides[n][0])
+            there, _, copy = copies[n]
+
+            @pl.when(there if where is None else there & where)
             def _(copy=copy):
                 copy.start()
 
-    def wait_halo(step, which):
+    def wait_halo(step, which, where=None):
         copies = halo_copies(step)
-        arrives = (has_xl, has_xh, has_yl, has_yh)
         for n in which:
-            copy = copies[n]
-
-            @pl.when(arrives[n])
+            _, arrives, copy = copies[n]
+
+            @pl.when(arrives if where is None else arrives & where)
             def _(copy=copy):
                 copy.wait_recv()
 
-            @pl.when(sides[n][0])
+    def drain_halo(step):
+        for there, _, copy in halo_copies(step):
+            @pl.when(there)
             def _(copy=copy):
                 copy.wait_send()
 
@@ -212,14 +217,15 @@
                 device_id=member(d), device_id_type=MESH,
             ).start()
 
-    def finish_sum(rnd):
-        every = pltpu.make_async_remote_copy(
+    def every(rnd):
+        return pltpu.make_async_remote_copy(
             src_ref=slots.at[rnd, 0 : devices - 1], dst_ref=slots.at[rnd, 0 : devices - 1],
             send_sem=sends.at[rnd], recv_sem=recvs.at[rnd],
             device_id=member(1), device_id_type=MESH,
         )
-        every.wait_recv()
-        every.wait_send()
+
+    def finish_sum(rnd):
+        every(rnd).wait_recv()
         return tree([slots[rnd, slot] for slot in range(devices)]) / cells
 
     shape = (padded_count, 128)
@@ -254,8 +260,9 @@
                 sums = (jnp.zeros((8, 128), jnp.float32),) * len(group)
             else:
                 sums = tuple(proj[kind, i] for i in group)
-            for start, stop in spans:
-                sums = lax.fori_loop(start // 8, stop // 8, step, sums, unroll=4)
+            for start, length in spans:
+                base = start // 8
+                sums = lax.fori_loop(0, length // 8, lambda r, s: step(base + r, s), sums, unroll=4)
             for i, acc in zip(group, sums):
                 proj[kind, i] = acc
 
@@ -292,8 +299,9 @@
                 piece(p, q)
 
     def combine(step, count, scale):
-        tall = 32 if rows_y % 32 == 0 else 16
+        tall = next(t for t in (64, 32, 16, 8) if rows_y % t == 0)
         scale_row = jnp.concatenate([scale] * (width // 128), axis=1)
+        more = step < STEPS - 1
 
         def plane(p):
             @pl.loop(0, rows_y // tall)
@@ -303,23 +311,22 @@
                 for i in range(count):
                     total = total - coef[i : i + 1, :] * vecs[i, at, :]
                 vecs[keep + step, at, :] = total
-                if step < STEPS - 1:
+                if more:
                     padded[step + 1, p + 2, pl.ds(pl.multiple_of(q * tall + 8, 8), tall), :] = total
 
-        more = step < STEPS - 1
-        done = []
-        for part, side in (((planes - 2, planes - 1), 0), ((0,), 1), (range(planes), 2)):
-            for p in part:
-                if p not in done:
-                    plane(p)
-                    done.append(p)
+        for p_even, p_odd, n_even, n_odd in (
+            (0, planes - 1, 2, 0),
+            (planes - 1, planes - 2, 0, 1),
+            (planes - 2, 0, 1, 2),
+        ):
+            plane(jnp.where(even, p_even, p_odd))
             if more:
-                start_halo(step + 1, (side,) if side < 2 else (2, 3))
-
-    def split(values):
-        scaled = values * 65537.0
-        high = scaled - (scaled - values)
-        return high, values - high
+                start_halo(step + 1, (n_even,), even)
+                start_halo(step + 1, (n_odd,), odd)
+        for p in range(1, planes - 2):
+            plane(p)
+        if more:
+            start_halo(step + 1, (3, 4))
 
     def outer(a, b):
         return lax.dot_general(
@@ -334,19 +341,27 @@
         values = vecs[0:keep, at, :].reshape(keep * 8, width)
         power = values * values
         squares[...] = squares[...] + power[:, :128] + power[:, 128:]
-        high, low = split(values)
+        high = values.astype(jnp.bfloat16)
+        low = (values - high.astype(jnp.float32)).astype(jnp.bfloat16)
         left = jnp.concatenate([high[:cut] * 0.5, high[cut:]], axis=0)
         first = outer(left, high[:cut]) + outer(low, high[:cut])
         second = outer(low, high[late:])
         third = outer(high[cut:] * 0.5, high[late:])
         return first, second, third
 
-    for copy in last_copies:
-        copy.wait()
-    start_halo(0, (0, 1, 2, 3))
-
     @pl.loop(0, chunks)
     def _(c):
+        @pl.when(c == 1)
+        def _():
+            pl.semaphore_wait(barrier, expected)
+            for d in range(1, n2):
+                pl.semaphore_signal(ready, inc=1, device_id=member2(d)[1], device_id_type=MESH)
+            for copy in last_copies:
+                copy.wait()
+            start_halo(0, (2, 0, 1), even)
+            start_halo(0, (0, 1, 2), odd)
+            start_halo(0, (3, 4))
+
         load(c).wait()
         found = [gram_block(c * CHUNK + s) for s in range(0, CHUNK, 8)]
         first, second, third = (functools.reduce(lambda a, b: a + b, f) for f in zip(*found))
@@ -364,31 +379,49 @@
     spread = jnp.concatenate([picked(head[...], 0), picked(tail[...], late)], axis=1)
     place = lax.broadcasted_iota(jnp.int32, (cut + 128, 128), 0)
     place = jnp.where(place < cut, place, place - cut + late) // 8
-    choose = (place == lax.broadcasted_iota(jnp.int32, place.shape, 1)).astype(jnp.float32)
-    exact = lax.Precision.HIGHEST
-    half = jnp.dot(spread, choose, precision=exact, preferred_element_type=jnp.float32)
-    turned = lax.dot_general(
-        choose, spread, (((0,), (1,)), ((), ())), precision=exact,
-        preferred_element_type=jnp.float32,
-    )
+    choose = jnp.where(place == lax.broadcasted_iota(jnp.int32, place.shape, 1), 1.0, 0.0)
+    choose = choose.astype(jnp.bfloat16)
+    half = jnp.zeros((keep, 128), jnp.float32)
+    for _ in range(3):
+        term = spread.astype(jnp.bfloat16)
+        spread = spread - term.astype(jnp.float32)
+        half = half + jnp.dot(term, choose, preferred_element_type=jnp.float32)
     diagonal = jnp.sum(jnp.sum(squares[...].reshape(keep, 8, 128), axis=1), axis=1, keepdims=True)
     lane_k = lax.broadcasted_iota(jnp.int32, (keep, 128), 1)
     sub_k = lax.broadcasted_iota(jnp.int32, (keep, 128), 0)
+    image[0:128, 0:128] = jnp.zeros((128, 128), jnp.float32)
     image[0:keep, 0:128] = half
-    image[0:128, 128:256] = jnp.zeros((128, 128), jnp.float32)
-    image[0:128, 128 : 128 + keep] = turned
-    both = half + image[0:keep, 128:256]
-    local_gram = jnp.where(lane_k == sub_k, diagonal, both)
-    slots1[me1] = jnp.zeros(slots1.shape[1:], jnp.float32)
-    slots1[me1, 0:keep] = local_gram
+    turned = jnp.transpose(image[0:128, 0:128])
+    pack[...] = jnp.zeros(pack.shape, jnp.float32)
+    pack[0:keep] = jnp.where(lane_k == sub_k, diagonal, half + turned[0:keep])
+    band = slots1.shape[1]
+    folded = jnp.zeros((band, 128), jnp.float32)
+    bands = [(g, g * band, min(g * band + band, padded_count)) for g in range(-(-padded_count // band))]
+    for g, start, stop in bands:
+        part = pack[start:stop]
+        if stop - start < band:
+            part = jnp.concatenate([part, jnp.zeros((band - stop + start, 128), jnp.float32)], axis=0)
+        folded = folded + (roll(part, g * padded_count, 1) if g else part)
+    slots1[me1] = folded
+
+    def unfold(values):
+        parts = [
+            (roll(values, 128 - g * padded_count, 1) if g else values)[0 : stop - start]
+            for g, start, stop in bands
+        ]
+        return jnp.where(lane < padded_count, jnp.concatenate(parts, axis=0), 0.0)
+
     react_copy.wait()
     exchange(stage1, True)
 
     everything = [(0, rows)]
-    inner = range(2, planes - 1)
-    edge = [p for p in range(planes) if p not in inner]
-    inner_spans = [(p * rows_y, (p + 1) * rows_y) for p in inner]
-    edge_spans = [(p * rows_y, (p + 1) * rows_y) for p in edge]
+
+    def span(p, n=1):
+        return [(p * rows_y, n * rows_y)]
+
+    def edge(step, p):
+        stencil(step, [p])
+        project(lambda at: image[at, :], keep + step, 0, span(p), False)
 
     def emit(step, scale):
         scale_row = jnp.concatenate([scale] * (width // 128), axis=1)
@@ -409,14 +442,17 @@
         if step > 0:
             project(lambda at: vecs[last, at, :], count, 1, everything, True)
             b_row = to_row(projected(1), eye_high)
-        wait_halo(step, (2, 3))
-        stencil(step, inner)
-        project(lambda at: image[at, :], count, 0, inner_spans, True)
+        wait_halo(step, (3, 4))
+        stencil(step, range(2, planes - 1))
+        project(lambda at: image[at, :], count, 0, span(2, planes - 3), True)
         if step > 1:
             emit(step - 2, scale)
-        wait_halo(step, (0, 1))
-        stencil(step, edge)
-        project(lambda at: image[at, :], count, 0, edge_spans, False)
+        wait_halo(step, (0,))
+        edge(step, 1)
+        for p_even, p_odd, n_even, n_odd in ((0, planes - 1, 1, 2), (planes - 1, 0, 2, 1)):
+            wait_halo(step, (n_even,), even)
+            wait_halo(step, (n_odd,), odd)
+            edge(step, jnp.where(even, p_even, p_odd))
         row = to_row(projected(0)) + b_row
         if step == 0:
             pl.semaphore_wait(ready, n2 - 1)
@@ -424,7 +460,7 @@
         if step == 0:
             slots2[me2] = exchange(stage1, False)
             exchange(stage2, True)
-            gram = exchange(stage2, False) / cells
+            gram = unfold(exchange(stage2, False) / cells)
             total = finish_sum(0)
         else:
             total = finish_sum(step)
@@ -458,6 +494,10 @@
     hess = jnp.where((sub8 == STEPS - 1) & (lane8 == last), norm, hess)
     h_out[...] = hess
     emit(STEPS - 1, 1.0 / norm)
+    for step in range(STEPS):
+        drain_halo(step)
+    for rnd in range(STEPS + 1):
+        every(rnd).wait_send()
 
 
 def group_of(count):
@@ -476,8 +516,13 @@
     padded_count = -(-size // 8) * 8
     rows = planes * rows_y
     rounds = STEPS + 1
+    band = -(-padded_count // (128 // padded_count) // 8) * 8
     f32 = jnp.float32
     dma = pltpu.SemaphoreType.DMA
+    held = [
+        pltpu.with_memory_space_constraint(x, pltpu.HBM)
+        for x in (basis_vectors.reshape(keep, rows, width), reaction.reshape(rows, width))
+    ]
     w, h = pl.pallas_call(
         functools.partial(kernel, keep, planes, rows_y, n_gx, n_gy, g1),
         out_shape=(
@@ -494,16 +539,17 @@
             pltpu.VMEM((keep * 8, 256), f32),
             pltpu.VMEM((keep * 8, 128), f32),
             pltpu.VMEM((keep * 8, 128), f32),
+            pltpu.VMEM((padded_count, 128), f32),
             pltpu.VMEM((2, padded_count, 8, 128), f32),
-            pltpu.VMEM((n1, padded_count, 128), f32),
-            pltpu.VMEM((n2, padded_count, 128), f32),
+            pltpu.VMEM((n1, band, 128), f32),
+            pltpu.VMEM((n2, band, 128), f32),
             pltpu.VMEM((rounds, n_gx * n_gy, 1, 128), f32),
             pltpu.VMEM((padded_count, width), f32),
             dma((rows // CHUNK,)),
             dma((planes,)),
             dma,
-            dma((STEPS, 4)),
-            dma((STEPS, 4)),
+            dma((STEPS, 5)),
+            dma((STEPS, 5)),
             dma((n1,)),
             dma((n1,)),
             dma((n2,)),
@@ -515,7 +561,7 @@
         compiler_params=pltpu.CompilerParams(
             collective_id=0, has_side_effects=True, vmem_limit_bytes=48 * 1024 * 1024
         ),
-    )(basis_vectors.reshape(keep, rows, width), reaction.reshape(rows, width))
+    )(*held)
     return w.reshape(STEPS, planes, rows_y, width), h[:STEPS, :size].T
 
 

time: 68.1 us -> 60.4 us (0.89)
  Pallas kernels: 64.8 us -> 58 us
  local copies, waits for them, and re-layouts: 2.49 us -> 1.55 us
    pallas_call x1, Pallas kernels: 64.8 us -> 58 us  [body(): pl.pallas_call(functools.partial(kernel, keep, planes, rows_y, n_gx, n_gy...]
    unnamed x3 -> x1, local copies, waits for them, and re-layouts: 1.91 us -> 0.97 us
where the time goes in v2:
time: 60.4 us; the launch traced here: 60.2 us
  Pallas kernels  58 us (96%)
  local copies, waits for them, and re-layouts  1.55 us (3%)
  between operations  0.64 us (1%)
    pallas_call x1, Pallas kernels, body(): pl.pallas_call(functools.partial(kernel, keep, planes, rows_y, n_gx, n_gy...  58 us

profile of v2, /device:TPU:0, one launch (start us, length us, event | category | flops | bytes accessed | tf_op | source)
XLA Modules:
  0.0 60.2 jit_solution(18441210797121471322)
XLA Ops:
  0.6 58.0 %shard_map.41 = (f32[4,256,256]{2,1,0:T(8,128)S(1)}, f32[8,128]{1,0:T(8,128)S(1)}) custom-call(f32[36,256,256]{2,1,0:T(8,128)} %bitcast.6, f32[256,256]{1,0:T(8,128)} %bitcast.7), custom_call_target="tpu_custom_call" | custom-call | tf_op jit(solution)/shard_map/pallas_call | solution.py:526
  58.6 0.6 slice_bitcast_fusion
  59.2 1.0 %copy.5 = f32[4,4,64,256]{3,2,1,0:T(8,128)} copy(f32[4,4,64,256]{3,2,1,0:T(8,128)S(1)} %bitcast.5) | data formatting | bytes 2097152

commit v3 on v2

--- a/solution.py
+++ b/solution.py
@@ -30,6 +30,39 @@
             for i in range(0, len(parts), 2)
         ]
     return parts[0]
+
+
+def two_sum(a, b):
+    total = a + b
+    other = total - a
+    return total, (a - (total - other)) + (b - other)
+
+
+def halves(a):
+    scaled = a * 4097.0
+    high = scaled - (scaled - a)
+    return high, a - high
+
+
+def two_product(a, b):
+    product = a * b
+    ah, al = halves(a)
+    bh, bl = halves(b)
+    return product, ((ah * bh - product) + ah * bl + al * bh) + al * bl
+
+
+def exact_tree(parts):
+    def add(a, b):
+        total, rest = two_sum(a[0], b[0])
+        return total, (a[1] + b[1]) + rest
+
+    pairs = [(part, jnp.zeros_like(part)) for part in parts]
+    while len(pairs) > 1:
+        pairs = [
+            add(pairs[i], pairs[i + 1]) if i + 1 < len(pairs) else pairs[i]
+            for i in range(0, len(pairs), 2)
+        ]
+    return pairs[0]
 
 
 def kernel(
@@ -206,7 +239,7 @@
             copy_of(member(d)[0], d).wait_recv()
         for d in range(1, count):
             copy_of(me, d).wait_send()
-        return tree([slots[slot] for slot in range(count)])
+        return [slots[slot] for slot in range(count)]
 
     def begin_sum(rnd, row):
         slots[rnd, me] = row
@@ -226,7 +259,8 @@
 
     def finish_sum(rnd):
         every(rnd).wait_recv()
-        return tree([slots[rnd, slot] for slot in range(devices)]) / cells
+        total, rest = exact_tree([slots[rnd, slot] for slot in range(devices)])
+        return total / cells, rest / cells
 
     shape = (padded_count, 128)
     lane = lax.broadcasted_iota(jnp.int32, shape, 1)
@@ -245,15 +279,17 @@
     def to_row(column, where=eye):
         return jnp.sum(jnp.where(where, column, 0.0), axis=0, keepdims=True)
 
-    def project(read, count, kind, spans, fresh):
-        for first in range(0, count, 20):
-            group = range(first, min(first + 20, count))
+    def project(read, count, kind, spans, fresh, square=False):
+        every_one = count + square
+        for first in range(0, every_one, 20):
+            group = range(first, min(first + 20, every_one))
 
             def step(r, sums):
                 at = pl.ds(pl.multiple_of(r * 8, 8), 8)
                 other = read(at)
                 return tuple(
-                    acc + fold_lanes(vecs[i, at, :] * other) for i, acc in zip(group, sums)
+                    acc + fold_lanes((vecs[i, at, :] if i < count else other) * other)
+                    for i, acc in zip(group, sums)
                 )
 
             if fresh:
@@ -298,9 +334,12 @@
             def _(q, p=p):
                 piece(p, q)
 
-    def combine(step, count, scale):
+    def widen(values):
+        return jnp.concatenate([values] * (width // 128), axis=1)
+
+    def combine(step, count, scale, inverse=None):
         tall = next(t for t in (64, 32, 16, 8) if rows_y % t == 0)
-        scale_row = jnp.concatenate([scale] * (width // 128), axis=1)
+        scale_row = widen(scale)
         more = step < STEPS - 1
 
         def plane(p):
@@ -310,9 +349,13 @@
                 total = image[at, :] * scale_row
                 for i in range(count):
                     total = total - coef[i : i + 1, :] * vecs[i, at, :]
-                vecs[keep + step, at, :] = total
                 if more:
+                    vecs[keep + step, at, :] = total
                     padded[step + 1, p + 2, pl.ds(pl.multiple_of(q * tall + 8, 8), tall), :] = total
+                else:
+                    w_out[step, at, :] = total * widen(inverse)
+                    if step > 0:
+                        w_out[step - 1, at, :] = vecs[keep + step - 1, at, :] * scale_row
 
         for p_even, p_odd, n_even, n_odd in (
             (0, planes - 1, 2, 0),
@@ -411,6 +454,16 @@
         ]
         return jnp.where(lane < padded_count, jnp.concatenate(parts, axis=0), 0.0)
 
+    def finish_gram():
+        total, rest = exact_tree(exchange(stage2, False))
+        row = lax.broadcasted_iota(jnp.int32, total.shape, 0)
+        column = lax.broadcasted_iota(jnp.int32, total.shape, 1)
+        ones = jnp.zeros(total.shape, jnp.float32)
+        for g, start, _ in bands:
+            on = (column == row + start + g * padded_count) & (row + start < keep)
+            ones = jnp.where(on, cells, ones)
+        return unfold(((ones - total) - rest) / cells)
+
     react_copy.wait()
     exchange(stage1, True)
 
@@ -421,21 +474,24 @@
 
     def edge(step, p):
         stencil(step, [p])
-        project(lambda at: image[at, :], keep + step, 0, span(p), False)
+        project(lambda at: image[at, :], keep + step, 0, span(p), False, step == STEPS - 1)
 
     def emit(step, scale):
-        scale_row = jnp.concatenate([scale] * (width // 128), axis=1)
+        scale_row = widen(scale)
 
         @pl.loop(0, rows // 32)
         def _(q):
             at = pl.ds(pl.multiple_of(q * 32, 32), 32)
             w_out[step, at, :] = vecs[keep + step, at, :] * scale_row
 
-    gram = None
+    gap = None
     scales = jnp.ones(shape, jnp.float32)
+    scales_row = jnp.ones((1, 128), jnp.float32)
+    lane1 = lax.broadcasted_iota(jnp.int32, (1, 128), 1)
     hess = jnp.zeros((8, 128), jnp.float32)
     b_row = jnp.zeros((1, 128), jnp.float32)
     scale = jnp.ones((1, 128), jnp.float32)
+    inverse = None
     for step in range(STEPS):
         count = keep + step
         last = count - 1
@@ -444,7 +500,7 @@
             b_row = to_row(projected(1), eye_high)
         wait_halo(step, (3, 4))
         stencil(step, range(2, planes - 1))
-        project(lambda at: image[at, :], count, 0, span(2, planes - 3), True)
+        project(lambda at: image[at, :], count, 0, span(2, planes - 3), True, step == STEPS - 1)
         if step > 1:
             emit(step - 2, scale)
         wait_halo(step, (0,))
@@ -458,46 +514,55 @@
             pl.semaphore_wait(ready, n2 - 1)
         begin_sum(step, row)
         if step == 0:
-            slots2[me2] = exchange(stage1, False)
+            slots2[me2] = tree(exchange(stage1, False))
             exchange(stage2, True)
-            gram = unfold(exchange(stage2, False) / cells)
-            total = finish_sum(0)
+            gap = finish_gram()
+            total, rest = finish_sum(0)
         else:
-            total = finish_sum(step)
+            total, rest = finish_sum(step)
             overlap = to_column(total, eye_high)
-            norm = jnp.sqrt(overlap[last : last + 1] + EPSILON)
+            length = overlap[last : last + 1]
+            length_rest = lane_sum(jnp.where(lane1 == 64 + last, rest, 0.0))
+            norm = jnp.sqrt(length + EPSILON)
             scale = 1.0 / norm
             hess = jnp.where((sub8 == step - 1) & (lane8 == last), norm, hess)
             scales = jnp.where(sub == last, scale, scales)
-            column = jnp.where(sub < count, overlap * scales * scale, 0.0)
-            gram = jnp.where(sub == last, to_row(column), gram)
-            gram = jnp.where(lane == last, column, gram)
+            scales_row = jnp.where(lane1 == last, scale, scales_row)
+            square, square_rest = two_product(scale, scale)
+            unit, unit_rest = two_product(length, square)
+            own = (((1.0 - unit) - unit_rest) - length * square_rest) - length_rest * square
+            column = jnp.where(sub < last, -overlap * scales * scale, 0.0)
+            column = jnp.where(sub == last, own, column)
+            gap = jnp.where(sub == last, to_row(column), gap)
+            gap = jnp.where(lane == last, column, gap)
         first = jnp.where(sub < count, to_column(total) * scales * scale, 0.0)
-        weights = first + (first - lane_sum(gram * to_row(first)))
-        weights = jnp.where(sub < count, weights, 0.0)
+        second = lane_sum(gap * to_row(first))
+        weights = jnp.where(sub < count, first + second, 0.0)
         scaled = weights * scales
-        coef[...] = jnp.concatenate([scaled] * (width // 128), axis=1)
-        combine(step, count, scale)
-        hess = jnp.where(sub8 == step, to_row(weights), hess)
-
-    last = keep + STEPS - 1
-
-    def square(r, acc):
-        values = vecs[last, pl.ds(pl.multiple_of(r * 8, 8), 8), :]
-        return acc + fold_lanes(values * values)
-
-    acc = lax.fori_loop(0, rows // 8, square, jnp.zeros((8, 128), jnp.float32), unroll=4)
-    begin_sum(STEPS, lane_sum(jnp.sum(acc, axis=0, keepdims=True)))
-    emit(STEPS - 2, scale)
-    total = finish_sum(STEPS)
-    norm = jnp.sqrt(total + EPSILON)
-    hess = jnp.where((sub8 == STEPS - 1) & (lane8 == last), norm, hess)
+        coef[...] = widen(scaled)
+        if step == STEPS - 1:
+            parts, parts_rest = two_product(total, scales_row)
+            parts_rest = parts_rest + rest * scales_row
+            power, power_rest = two_product(parts, parts)
+            power_rest = power_rest + 2.0 * parts * parts_rest
+            whole = jnp.where(lane1 == count, total, 0.0)
+            power = jnp.where(lane1 < count, power, -whole)
+            power_rest = jnp.where(lane1 < count, power_rest, jnp.where(lane1 == count, -rest, 0.0))
+            grid = lane_sum(whole) * 128.0
+            coarse = (power + grid) - grid
+            left = -(lane_sum(coarse) + lane_sum((power - coarse) + power_rest))
+            third = lane_sum(gap * to_row(second))
+            left = left * scale * scale - jnp.sum(first * second + weights * third, axis=0, keepdims=True)
+            norm = jnp.sqrt(jnp.maximum(left, 0.0) + EPSILON)
+            inverse = 1.0 / norm
+            hess = jnp.where((sub8 == step) & (lane8 == count), norm, hess)
+        combine(step, count, scale, inverse)
+        hess = jnp.where((sub8 == step) & (lane8 < count), to_row(weights), hess)
+
     h_out[...] = hess
-    emit(STEPS - 1, 1.0 / norm)
     for step in range(STEPS):
         drain_halo(step)
-    for rnd in range(STEPS + 1):
-        every(rnd).wait_send()
+        every(step).wait_send()
 
 
 def group_of(count):
@@ -515,7 +580,7 @@
     size = keep + STEPS
     padded_count = -(-size // 8) * 8
     rows = planes * rows_y
-    rounds = STEPS + 1
+    rounds = STEPS
     band = -(-padded_count // (128 // padded_count) // 8) * 8
     f32 = jnp.float32
     dma = pltpu.SemaphoreType.DMA

time: 60.4 us -> 55.6 us (0.921)
  Pallas kernels: 58 us -> 53.3 us
    pallas_call x1, Pallas kernels: 58 us -> 53.3 us  [body(): pl.pallas_call(functools.partial(kernel, keep, planes, rows_y, n_gx, n_gy...]
where the time goes in v3:
time: 55.6 us; the launch traced here: 55.4 us
  Pallas kernels  53.3 us (96%)
  local copies, waits for them, and re-layouts  1.55 us (3%)
  between operations  0.64 us (1%)
    pallas_call x1, Pallas kernels, body(): pl.pallas_call(functools.partial(kernel, keep, planes, rows_y, n_gx, n_gy...  53.3 us

profile of v3, /device:TPU:0, one launch (start us, length us, event | category | flops | bytes accessed | tf_op | source)
XLA Modules:
  0.0 55.4 jit_solution(1024078462613746451)
XLA Ops:
  0.6 53.3 %shard_map.41 = (f32[4,256,256]{2,1,0:T(8,128)S(1)}, f32[8,128]{1,0:T(8,128)S(1)}) custom-call(f32[36,256,256]{2,1,0:T(8,128)} %bitcast.6, f32[256,256]{1,0:T(8,128)} %bitcast.7), custom_call_target="tpu_custom_call" | custom-call | tf_op jit(solution)/shard_map/pallas_call | solution.py:591
  53.9 0.6 %slice_bitcast_fusion = f32[40,4]{0,1:T(4,128)} fusion(f32[8,128]{1,0:T(8,128)S(1)} %get-tuple-element.5), kind=kLoop, calls=%fused_computation | loop fusion | bytes 1280 | tf_op jit(solution)/shard_map/transpose | solution.py:630
  54.5 1.0 %copy.5 = f32[4,4,64,256]{3,2,1,0:T(8,128)} copy(f32[4,4,64,256]{3,2,1,0:T(8,128)S(1)} %bitcast.5) | data formatting | bytes 2097152

commit v4 on v3

--- a/solution.py
+++ b/solution.py
@@ -122,8 +122,14 @@
     me = gx * n_gy + gy
     devices = n_gx * n_gy
 
+    bits = devices.bit_length() - 1
+    turns = [(1 - 2 * lax.rem(me // 2**i, 2)) * 2**i for i in range(bits)]
+
     def member(d):
-        p = lax.rem(me + d, devices)
+        if devices == 2**bits:
+            p = me + functools.reduce(lambda a, b: a + b, [t for i, t in enumerate(turns) if d >> i & 1])
+        else:
+            p = lax.rem(me + d, devices)
         return {"gx": p // n_gy, "gy": lax.rem(p, n_gy)}
 
     barrier = pltpu.get_barrier_semaphore()
@@ -171,16 +177,19 @@
     tail[...] = jnp.zeros(tail.shape, jnp.float32)
     squares[...] = jnp.zeros(squares.shape, jnp.float32)
     proj[...] = jnp.zeros(proj.shape, jnp.float32)
+    rows_half = rows_y // 2
+
     def halo_copies(step):
         own = pl.ds(2, planes)
-        inside = slice(8, rows_y + 8)
-        refs = (
-            (0, padded.at[step, planes + 1, inside], padded.at[step, 1, inside]),
-            (0, padded.at[step, planes, inside], padded.at[step, 0, inside]),
-            (1, padded.at[step, 2, inside], padded.at[step, planes + 2, inside]),
+        part = [slice(8 + h * rows_half, 8 + (h + 1) * rows_half) for h in range(2)]
+        refs = [
+            (side, padded.at[step, src, at], padded.at[step, dst, at])
+            for side, src, dst in ((0, planes + 1, 1), (0, planes, 0), (1, 2, planes + 2))
+            for at in part
+        ] + [
             (2, padded.at[step, own, rows_y : rows_y + 8], padded.at[step, own, 0:8]),
             (3, padded.at[step, own, 8:16], padded.at[step, own, rows_y + 8 : rows_y + 16]),
-        )
+        ]
         return [
             (
                 sides[side][0],
@@ -243,7 +252,7 @@
 
     def begin_sum(rnd, row):
         slots[rnd, me] = row
-        for d in range(1, devices):
+        for d in range(devices - 1, 0, -1):
             pltpu.make_async_remote_copy(
                 src_ref=slots.at[rnd, me], dst_ref=slots.at[rnd, me],
                 send_sem=sends.at[rnd], recv_sem=recvs.at[rnd],
@@ -302,6 +311,28 @@
             for i, acc in zip(group, sums):
                 proj[kind, i] = acc
 
+    def project_late(step, count, p, halo, factor, h):
+        square = step == STEPS - 1
+        every_one = count + square
+        for first in range(0, every_one, 20):
+            group = range(first, min(first + 20, every_one))
+
+            def add(r, sums):
+                at = pl.ds(pl.multiple_of(p * rows_y + h * rows_half + r * 8, 8), 8)
+                other = padded[step, halo, pl.ds(pl.multiple_of(8 + h * rows_half + r * 8, 8), 8), :] * factor
+                whole = other
+                if every_one in (group.stop,):
+                    whole = image[at, :] + other
+                    image[at, :] = whole
+                return tuple(
+                    acc + fold_lanes(vecs[i, at, :] * other if i < count else whole * whole)
+                    for i, acc in zip(group, sums)
+                )
+
+            sums = lax.fori_loop(0, rows_half // 8, add, tuple(proj[0, i] for i in group), unroll=True)
+            for i, acc in zip(group, sums):
+                proj[0, i] = acc
+
     def projected(kind):
         return lane_sum(jnp.sum(proj[kind], axis=1))
 
@@ -318,9 +349,9 @@
             here = block[8 : tall + 8]
             out_at = pl.ds(pl.multiple_of(p * rows_y + base, 8), tall)
             total = -(react[out_at, :] + centre) * here
-            total = total + padded[step, p + 3, at, :]
+            total = total + padded[step, p + 3, at, :] if p < planes - 1 else total
             total = total + (1.0 + 2.0 * sx) * padded[step, p + 1, at, :]
-            total = total - (0.5 * sx) * padded[step, p, at, :]
+            total = total - (0.5 * sx) * padded[step, p, at, :] if p > 0 else total
             total = total + roll(block, tall + 15, 0)[8 : tall + 8]
             total = total + (1.0 + 2.0 * sy) * roll(block, 1, 0)[8 : tall + 8]
             total = total - (0.5 * sy) * roll(block, 2, 0)[8 : tall + 8]
@@ -338,38 +369,40 @@
         return jnp.concatenate([values] * (width // 128), axis=1)
 
     def combine(step, count, scale, inverse=None):
-        tall = next(t for t in (64, 32, 16, 8) if rows_y % t == 0)
         scale_row = widen(scale)
         more = step < STEPS - 1
 
-        def plane(p):
-            @pl.loop(0, rows_y // tall)
-            def _(q):
-                at = pl.ds(pl.multiple_of(p * rows_y + q * tall, 8), tall)
-                total = image[at, :] * scale_row
-                for i in range(count):
-                    total = total - coef[i : i + 1, :] * vecs[i, at, :]
+        def plane(p, start, tall):
+            at = pl.ds(pl.multiple_of(p * rows_y + start, 8), tall)
+            total = image[at, :] * scale_row
+            for i in range(count):
+                total = total - coef[i : i + 1, :] * vecs[i, at, :]
+            if more:
+                vecs[keep + step, at, :] = total
+                padded[step + 1, p + 2, start + 8 : start + 8 + tall, :] = total
+            else:
+                w_out[step, at, :] = total * widen(inverse)
+                if step > 0:
+                    w_out[step - 1, at, :] = vecs[keep + step - 1, at, :] * scale_row
+
+        for n, (p_even, p_odd, n_even, n_odd) in enumerate((
+            (0, planes - 1, 4, 0),
+            (planes - 1, planes - 2, 0, 2),
+            (planes - 2, 0, 2, 4),
+        )):
+            p = jnp.where(even, p_even, p_odd)
+            if n > 0:
+                plane(p, 0, rows_y)
+            for h in range(2):
+                if n == 0:
+                    plane(p, h * rows_half, rows_half)
                 if more:
-                    vecs[keep + step, at, :] = total
-                    padded[step + 1, p + 2, pl.ds(pl.multiple_of(q * tall + 8, 8), tall), :] = total
-                else:
-                    w_out[step, at, :] = total * widen(inverse)
-                    if step > 0:
-                        w_out[step - 1, at, :] = vecs[keep + step - 1, at, :] * scale_row
-
-        for p_even, p_odd, n_even, n_odd in (
-            (0, planes - 1, 2, 0),
-            (planes - 1, planes - 2, 0, 1),
-            (planes - 2, 0, 1, 2),
-        ):
-            plane(jnp.where(even, p_even, p_odd))
-            if more:
-                start_halo(step + 1, (n_even,), even)
-                start_halo(step + 1, (n_odd,), odd)
+                    start_halo(step + 1, (n_even + h,), even)
+                    start_halo(step + 1, (n_odd + h,), odd)
         for p in range(1, planes - 2):
-            plane(p)
+            plane(p, 0, rows_y)
         if more:
-            start_halo(step + 1, (3, 4))
+            start_halo(step + 1, (6, 7))
 
     def outer(a, b):
         return lax.dot_general(
@@ -401,9 +434,9 @@
                 pl.semaphore_signal(ready, inc=1, device_id=member2(d)[1], device_id_type=MESH)
             for copy in last_copies:
                 copy.wait()
-            start_halo(0, (2, 0, 1), even)
-            start_halo(0, (0, 1, 2), odd)
-            start_halo(0, (3, 4))
+            start_halo(0, (4, 5, 0, 1, 2, 3), even)
+            start_halo(0, (0, 1, 2, 3, 4, 5), odd)
+            start_halo(0, (6, 7))
 
         load(c).wait()
         found = [gram_block(c * CHUNK + s) for s in range(0, CHUNK, 8)]
@@ -472,9 +505,14 @@
     def span(p, n=1):
         return [(p * rows_y, n * rows_y)]
 
-    def edge(step, p):
-        stencil(step, [p])
-        project(lambda at: image[at, :], keep + step, 0, span(p), False, step == STEPS - 1)
+    def project_image(step, spans, fresh=False, square=False):
+        project(lambda at: image[at, :], keep + step, 0, spans, fresh, square)
+
+    sx = WIND_SPEEDS[0]
+    order = (
+        [(0, 0, -0.5 * sx, h, 2 + h) for h in range(2)],
+        [(planes - 1, planes + 2, 1.0, h, 4 + h) for h in range(2)],
+    )
 
     def emit(step, scale):
         scale_row = widen(scale)
@@ -498,27 +536,34 @@
         if step > 0:
             project(lambda at: vecs[last, at, :], count, 1, everything, True)
             b_row = to_row(projected(1), eye_high)
-        wait_halo(step, (3, 4))
-        stencil(step, range(2, planes - 1))
-        project(lambda at: image[at, :], count, 0, span(2, planes - 3), True, step == STEPS - 1)
+        square = step == STEPS - 1
+        wait_halo(step, (6, 7))
+        stencil(step, range(2, planes))
+        project_image(step, span(2, planes - 3), True, square)
+        project_image(step, span(planes - 1))
         if step > 1:
             emit(step - 2, scale)
-        wait_halo(step, (0,))
-        edge(step, 1)
-        for p_even, p_odd, n_even, n_odd in ((0, planes - 1, 1, 2), (planes - 1, 0, 2, 1)):
-            wait_halo(step, (n_even,), even)
-            wait_halo(step, (n_odd,), odd)
-            edge(step, jnp.where(even, p_even, p_odd))
+        wait_halo(step, (0, 1))
+        stencil(step, range(2))
+        project_image(step, span(0))
+        project_image(step, span(1), False, square)
+        for first, second in zip(order[0] + order[1], order[1] + order[0]):
+            wait_halo(step, (first[4],), even)
+            wait_halo(step, (second[4],), odd)
+            p, halo, factor = (jnp.where(even, a, b) for a, b in zip(first[:3], second[:3]))
+            project_late(step, count, p, halo, factor, first[3])
         row = to_row(projected(0)) + b_row
         if step == 0:
             pl.semaphore_wait(ready, n2 - 1)
         begin_sum(step, row)
+        drain_halo(step)
         if step == 0:
             slots2[me2] = tree(exchange(stage1, False))
             exchange(stage2, True)
             gap = finish_gram()
             total, rest = finish_sum(0)
         else:
+            every(step - 1).wait_send()
             total, rest = finish_sum(step)
             overlap = to_column(total, eye_high)
             length = overlap[last : last + 1]
@@ -556,13 +601,12 @@
             norm = jnp.sqrt(jnp.maximum(left, 0.0) + EPSILON)
             inverse = 1.0 / norm
             hess = jnp.where((sub8 == step) & (lane8 == count), norm, hess)
+        hess = jnp.where((sub8 == step) & (lane8 < count), to_row(weights), hess)
+        if step == STEPS - 1:
+            h_out[...] = hess
         combine(step, count, scale, inverse)
-        hess = jnp.where((sub8 == step) & (lane8 < count), to_row(weights), hess)
-
-    h_out[...] = hess
-    for step in range(STEPS):
-        drain_halo(step)
-        every(step).wait_send()
+
+    every(STEPS - 1).wait_send()
 
 
 def group_of(count):
@@ -613,8 +657,8 @@
             dma((rows // CHUNK,)),
             dma((planes,)),
             dma,
-            dma((STEPS, 5)),
-            dma((STEPS, 5)),
+            dma((STEPS, 8)),
+            dma((STEPS, 8)),
             dma((n1,)),
             dma((n1,)),
             dma((n2,)),

time: 55.6 us -> 55 us (0.989)
  Pallas kernels: 53.3 us -> 52.6 us
    pallas_call x1, Pallas kernels: 53.3 us -> 52.6 us  [body(): pl.pallas_call(functools.partial(kernel, keep, planes, rows_y, n_gx, n_gy...]
where the time goes in v4:
time: 55 us; the launch traced here: 54.8 us
  Pallas kernels  52.6 us (96%)
  local copies, waits for them, and re-layouts  1.55 us (3%)
  between operations  0.64 us (1%)
    pallas_call x1, Pallas kernels, body(): pl.pallas_call(functools.partial(kernel, keep, planes, rows_y, n_gx, n_gy...  52.6 us

profile of v4, /device:TPU:0, one launch (start us, length us, event | category | flops | bytes accessed | tf_op | source)
XLA Modules:
  0.0 54.8 jit_solution(2793588006278628811)
XLA Ops:
  0.6 52.6 %shard_map.41 = (f32[4,256,256]{2,1,0:T(8,128)S(1)}, f32[8,128]{1,0:T(8,128)S(1)}) custom-call(f32[36,256,256]{2,1,0:T(8,128)} %bitcast.6, f32[256,256]{1,0:T(8,128)} %bitcast.7), custom_call_target="tpu_custom_call" | custom-call | tf_op jit(solution)/shard_map/pallas_call | solution.py:635
  53.3 0.6 %slice_bitcast_fusion = f32[40,4]{0,1:T(4,128)} fusion(f32[8,128]{1,0:T(8,128)S(1)} %get-tuple-element.5), kind=kLoop, calls=%fused_computation | loop fusion | bytes 1280 | tf_op jit(solution)/shard_map/transpose | solution.py:674
  53.9 1.0 %copy.5 = f32[4,4,64,256]{3,2,1,0:T(8,128)} copy(f32[4,4,64,256]{3,2,1,0:T(8,128)S(1)} %bitcast.5) | data formatting | bytes 2097152

commit v5 on v4

--- a/solution.py
+++ b/solution.py
@@ -89,12 +89,13 @@
         pltpu.make_async_copy(
             basis.at[keep - 1, p * rows_y : (p + 1) * rows_y],
             padded.at[0, p + 2, 8 : rows_y + 8],
-            last_sem.at[p],
+            last_sem,
         )
         for p in range(planes)
     ]
     for copy in last_copies:
         copy.start()
+    all_last = padded.at[0, 2 : planes + 2, 8 : rows_y + 8]
     chunks = rows // CHUNK
 
     def load(c):
@@ -196,7 +197,7 @@
                 (has_xl, has_xh, has_yl, has_yh)[side],
                 pltpu.make_async_remote_copy(
                     src_ref=src, dst_ref=dst,
-                    send_sem=halo_send.at[step, n], recv_sem=halo_recv.at[step, n],
+                    send_sem=halo_send.at[side], recv_sem=halo_recv.at[n],
                     device_id=sides[side][1], device_id_type=MESH,
                 ),
             )
@@ -222,7 +223,22 @@
                 copy.wait_recv()
 
     def drain_halo(step):
-        for there, _, copy in halo_copies(step):
+        inside = slice(8, rows_y + 8)
+        copies = halo_copies(step)
+        groups = (
+            padded.at[step, planes : planes + 2, inside],
+            padded.at[step, 2:3, inside],
+        )
+        for side, group in enumerate(groups):
+            @pl.when(sides[side][0])
+            def _(side=side, group=group):
+                pltpu.make_async_remote_copy(
+                    src_ref=group, dst_ref=group,
+                    send_sem=halo_send.at[side], recv_sem=halo_recv.at[0],
+                    device_id=sides[side][1], device_id_type=MESH,
+                ).wait_send()
+
+        for there, _, copy in copies[6:]:
             @pl.when(there)
             def _(copy=copy):
                 copy.wait_send()
@@ -233,10 +249,9 @@
     def exchange(stage, begin):
         slots, me, count, member, send, recv = stage
 
-        def copy_of(slot, d):
+        def copy_of(at, d):
             return pltpu.make_async_remote_copy(
-                src_ref=slots.at[slot], dst_ref=slots.at[slot],
-                send_sem=send.at[d - 1], recv_sem=recv.at[slot],
+                src_ref=slots.at[at], dst_ref=slots.at[at], send_sem=send, recv_sem=recv,
                 device_id=member(d)[1], device_id_type=MESH,
             )
 
@@ -244,10 +259,10 @@
             for d in range(1, count):
                 copy_of(me, d).start()
             return None
-        for d in range(1, count):
-            copy_of(member(d)[0], d).wait_recv()
-        for d in range(1, count):
-            copy_of(me, d).wait_send()
+        if count > 1:
+            every_copy = copy_of(pl.ds(0, count - 1), 1)
+            every_copy.wait_recv()
+            every_copy.wait_send()
         return [slots[slot] for slot in range(count)]
 
     def begin_sum(rnd, row):
@@ -255,19 +270,20 @@
         for d in range(devices - 1, 0, -1):
             pltpu.make_async_remote_copy(
                 src_ref=slots.at[rnd, me], dst_ref=slots.at[rnd, me],
-                send_sem=sends.at[rnd], recv_sem=recvs.at[rnd],
+                send_sem=sends, recv_sem=recvs.at[rnd % 2],
                 device_id=member(d), device_id_type=MESH,
             ).start()
 
     def every(rnd):
         return pltpu.make_async_remote_copy(
             src_ref=slots.at[rnd, 0 : devices - 1], dst_ref=slots.at[rnd, 0 : devices - 1],
-            send_sem=sends.at[rnd], recv_sem=recvs.at[rnd],
+            send_sem=sends, recv_sem=recvs.at[rnd % 2],
             device_id=member(1), device_id_type=MESH,
         )
 
     def finish_sum(rnd):
         every(rnd).wait_recv()
+        every(rnd).wait_send()
         total, rest = exact_tree([slots[rnd, slot] for slot in range(devices)])
         return total / cells, rest / cells
 
@@ -432,8 +448,7 @@
             pl.semaphore_wait(barrier, expected)
             for d in range(1, n2):
                 pl.semaphore_signal(ready, inc=1, device_id=member2(d)[1], device_id_type=MESH)
-            for copy in last_copies:
-                copy.wait()
+            pltpu.make_async_copy(all_last, all_last, last_sem).wait()
             start_halo(0, (4, 5, 0, 1, 2, 3), even)
             start_halo(0, (0, 1, 2, 3, 4, 5), odd)
             start_halo(0, (6, 7))
@@ -563,7 +578,6 @@
             gap = finish_gram()
             total, rest = finish_sum(0)
         else:
-            every(step - 1).wait_send()
             total, rest = finish_sum(step)
             overlap = to_column(total, eye_high)
             length = overlap[last : last + 1]
@@ -606,8 +620,6 @@
             h_out[...] = hess
         combine(step, count, scale, inverse)
 
-    every(STEPS - 1).wait_send()
-
 
 def group_of(count):
     for size in (4, 2):
@@ -655,16 +667,16 @@
             pltpu.VMEM((rounds, n_gx * n_gy, 1, 128), f32),
             pltpu.VMEM((padded_count, width), f32),
             dma((rows // CHUNK,)),
-            dma((planes,)),
             dma,
-            dma((STEPS, 8)),
-            dma((STEPS, 8)),
-            dma((n1,)),
-            dma((n1,)),
-            dma((n2,)),
-            dma((n2,)),
-            dma((rounds,)),
-            dma((rounds,)),
+            dma,
+            dma((4,)),
+            dma((8,)),
+            dma,
+            dma,
+            dma,
+            dma,
+            dma,
+            dma((2,)),
             pltpu.SemaphoreType.REGULAR,
         ],
         compiler_params=pltpu.CompilerParams(

time: 55 us -> 54.3 us (0.987)
  Pallas kernels: 52.6 us -> 51.9 us
    pallas_call x1, Pallas kernels: 52.6 us -> 51.9 us  [body(): pl.pallas_call(functools.partial(kernel, keep, planes, rows_y, n_gx, n_gy...]
where the time goes in v5:
time: 54.3 us; the launch traced here: 54.1 us
  Pallas kernels  51.9 us (96%)
  local copies, waits for them, and re-layouts  1.55 us (3%)
  between operations  0.64 us (1%)
    pallas_call x1, Pallas kernels, body(): pl.pallas_call(functools.partial(kernel, keep, planes, rows_y, n_gx, n_gy...  51.9 us

profile of v5, /device:TPU:0, one launch (start us, length us, event | category | flops | bytes accessed | tf_op | source)
XLA Modules:
  0.0 54.1 jit_solution(14602640994194228142)
XLA Ops:
  0.6 51.9 %shard_map.41 = (f32[4,256,256]{2,1,0:T(8,128)S(1)}, f32[8,128]{1,0:T(8,128)S(1)}) custom-call(f32[36,256,256]{2,1,0:T(8,128)} %bitcast.6, f32[256,256]{1,0:T(8,128)} %bitcast.7), custom_call_target="tpu_custom_call" | custom-call | tf_op jit(solution)/shard_map/pallas_call | solution.py:647
  52.5 0.6 %slice_bitcast_fusion = f32[40,4]{0,1:T(4,128)} fusion(f32[8,128]{1,0:T(8,128)S(1)} %get-tuple-element.5), kind=kLoop, calls=%fused_computation | loop fusion | bytes 1280 | tf_op jit(solution)/shard_map/transpose | solution.py:686
  53.1 1.0 %copy.5 = f32[4,4,64,256]{3,2,1,0:T(8,128)} copy(f32[4,4,64,256]{3,2,1,0:T(8,128)S(1)} %bitcast.5) | data formatting | bytes 2097152

commit v6 on v5

--- a/solution.py
+++ b/solution.py
@@ -21,15 +21,6 @@
 def fold_lanes(values):
     parts = [values[:, s : s + 128] for s in range(0, values.shape[1], 128)]
     return functools.reduce(lambda a, b: a + b, parts)
-
-
-def tree(parts):
-    while len(parts) > 1:
-        parts = [
-            parts[i] + parts[i + 1] if i + 1 < len(parts) else parts[i]
-            for i in range(0, len(parts), 2)
-        ]
-    return parts[0]
 
 
 def two_sum(a, b):
@@ -68,9 +59,9 @@
 def kernel(
     keep, planes, rows_y, n_gx, n_gy, g1,
     basis, reaction, w_out, h_out,
-    vecs, padded, image, react, head, tail, squares, pack, proj, slots1, slots2, slots, coef,
+    vecs, padded, image, react, head, tail, squares, pack, proj, grams, slots, coef,
     load_sem, last_sem, react_sem,
-    halo_send, halo_recv, send1, recv1, send2, recv2, sends, recvs, ready,
+    halo_send, halo_recv, gram_send, gram_recv, sends, recvs, ready,
 ):
     width = basis.shape[2]
     rows = planes * rows_y
@@ -243,27 +234,11 @@
             def _(copy=copy):
                 copy.wait_send()
 
-    stage1 = (slots1, me1, n1, member1, send1, recv1)
-    stage2 = (slots2, me2, n2, member2, send2, recv2)
-
-    def exchange(stage, begin):
-        slots, me, count, member, send, recv = stage
-
-        def copy_of(at, d):
-            return pltpu.make_async_remote_copy(
-                src_ref=slots.at[at], dst_ref=slots.at[at], send_sem=send, recv_sem=recv,
-                device_id=member(d)[1], device_id_type=MESH,
-            )
-
-        if begin:
-            for d in range(1, count):
-                copy_of(me, d).start()
-            return None
-        if count > 1:
-            every_copy = copy_of(pl.ds(0, count - 1), 1)
-            every_copy.wait_recv()
-            every_copy.wait_send()
-        return [slots[slot] for slot in range(count)]
+    def gram_copy(at, d):
+        return pltpu.make_async_remote_copy(
+            src_ref=grams.at[at], dst_ref=grams.at[at], send_sem=gram_send, recv_sem=gram_recv,
+            device_id=member(d), device_id_type=MESH,
+        )
 
     def begin_sum(rnd, row):
         slots[rnd, me] = row
@@ -480,40 +455,44 @@
     diagonal = jnp.sum(jnp.sum(squares[...].reshape(keep, 8, 128), axis=1), axis=1, keepdims=True)
     lane_k = lax.broadcasted_iota(jnp.int32, (keep, 128), 1)
     sub_k = lax.broadcasted_iota(jnp.int32, (keep, 128), 0)
-    image[0:128, 0:128] = jnp.zeros((128, 128), jnp.float32)
-    image[0:keep, 0:128] = half
-    turned = jnp.transpose(image[0:128, 0:128])
     pack[...] = jnp.zeros(pack.shape, jnp.float32)
+    pack[0:keep] = half
+    turned = jnp.transpose(pack[...])
     pack[0:keep] = jnp.where(lane_k == sub_k, diagonal, half + turned[0:keep])
-    band = slots1.shape[1]
-    folded = jnp.zeros((band, 128), jnp.float32)
-    bands = [(g, g * band, min(g * band + band, padded_count)) for g in range(-(-padded_count // band))]
-    for g, start, stop in bands:
-        part = pack[start:stop]
-        if stop - start < band:
-            part = jnp.concatenate([part, jnp.zeros((band - stop + start, 128), jnp.float32)], axis=0)
-        folded = folded + (roll(part, g * padded_count, 1) if g else part)
-    slots1[me1] = folded
-
-    def unfold(values):
-        parts = [
-            (roll(values, 128 - g * padded_count, 1) if g else values)[0 : stop - start]
-            for g, start, stop in bands
-        ]
-        return jnp.where(lane < padded_count, jnp.concatenate(parts, axis=0), 0.0)
+    blocks, start = [], 0
+    for b in range(0, keep, 8):
+        blocks.append((b, start))
+        start += keep - b
+    folded = jnp.zeros((8, 128), jnp.float32)
+    for b, start in blocks:
+        part = jnp.where((lane8 >= b) & (lane8 < keep), pack[b : b + 8], 0.0)
+        folded = folded + (roll(part, start - b, 1) if start > b else part)
+    grams[me] = folded
+    pl.semaphore_wait(ready, n2 - 1)
+    for d in range(devices - 1, 0, -1):
+        gram_copy(me, d).start()
 
     def finish_gram():
-        total, rest = exact_tree(exchange(stage2, False))
-        row = lax.broadcasted_iota(jnp.int32, total.shape, 0)
-        column = lax.broadcasted_iota(jnp.int32, total.shape, 1)
-        ones = jnp.zeros(total.shape, jnp.float32)
-        for g, start, _ in bands:
-            on = (column == row + start + g * padded_count) & (row + start < keep)
-            ones = jnp.where(on, cells, ones)
-        return unfold(((ones - total) - rest) / cells)
+        arrived = gram_copy(pl.ds(0, devices - 1), 1)
+        arrived.wait_recv()
+        arrived.wait_send()
+        total, rest = exact_tree([grams[slot] for slot in range(devices)])
+        ones = jnp.zeros((8, 128), jnp.float32)
+        for b, start in blocks:
+            ones = jnp.where((lane8 == sub8 + start) & (sub8 + b < keep), cells, ones)
+        values = ((ones - total) - rest) / cells
+        parts = []
+        for b, start in blocks:
+            part = roll(values, 128 + b - start, 1) if start > b else values
+            parts.append(jnp.where((lane8 >= b) & (lane8 < keep), part, 0.0))
+        upper = jnp.concatenate(parts, axis=0)
+        pack[0 : 8 * len(parts)] = upper
+        lower = jnp.transpose(pack[...])[0 : 8 * len(parts)]
+        rows_of = lax.broadcasted_iota(jnp.int32, upper.shape, 0) // 8
+        lanes_of = lax.broadcasted_iota(jnp.int32, upper.shape, 1) // 8
+        return upper + jnp.where(rows_of > lanes_of, lower, 0.0)
 
     react_copy.wait()
-    exchange(stage1, True)
 
     everything = [(0, rows)]
 
@@ -568,13 +547,9 @@
             p, halo, factor = (jnp.where(even, a, b) for a, b in zip(first[:3], second[:3]))
             project_late(step, count, p, halo, factor, first[3])
         row = to_row(projected(0)) + b_row
-        if step == 0:
-            pl.semaphore_wait(ready, n2 - 1)
         begin_sum(step, row)
         drain_halo(step)
         if step == 0:
-            slots2[me2] = tree(exchange(stage1, False))
-            exchange(stage2, True)
             gap = finish_gram()
             total, rest = finish_sum(0)
         else:
@@ -632,12 +607,10 @@
     keep, planes, rows_y, width = basis_vectors.shape
     n_gx, n_gy = lax.axis_size("gx"), lax.axis_size("gy")
     g1 = group_of(n_gx)
-    n1, n2 = g1 * n_gy, n_gx // g1
     size = keep + STEPS
     padded_count = -(-size // 8) * 8
     rows = planes * rows_y
     rounds = STEPS
-    band = -(-padded_count // (128 // padded_count) // 8) * 8
     f32 = jnp.float32
     dma = pltpu.SemaphoreType.DMA
     held = [
@@ -660,10 +633,9 @@
             pltpu.VMEM((keep * 8, 256), f32),
             pltpu.VMEM((keep * 8, 128), f32),
             pltpu.VMEM((keep * 8, 128), f32),
-            pltpu.VMEM((padded_count, 128), f32),
+            pltpu.VMEM((128, 128), f32),
             pltpu.VMEM((2, padded_count, 8, 128), f32),
-            pltpu.VMEM((n1, band, 128), f32),
-            pltpu.VMEM((n2, band, 128), f32),
+            pltpu.VMEM((n_gx * n_gy, 8, 128), f32),
             pltpu.VMEM((rounds, n_gx * n_gy, 1, 128), f32),
             pltpu.VMEM((padded_count, width), f32),
             dma((rows // CHUNK,)),
@@ -671,8 +643,6 @@
             dma,
             dma((4,)),
             dma((8,)),
-            dma,
-            dma,
             dma,
             dma,
             dma,

time: 54.3 us -> 54 us (level)
  no operation moved by 1% of the time
where the time goes in v6:
time: 54 us; the launch traced here: 53.8 us
  Pallas kernels  51.7 us (96%)
  local copies, waits for them, and re-layouts  1.55 us (3%)
  between operations  0.64 us (1%)
    pallas_call x1, Pallas kernels, body(): pl.pallas_call(functools.partial(kernel, keep, planes, rows_y, n_gx, n_gy...  51.7 us

profile of v6, /device:TPU:0, one launch (start us, length us, event | category | flops | bytes accessed | tf_op | source)
XLA Modules:
  0.0 53.8 jit_solution(8989043500516108391)
XLA Ops:
  0.6 51.7 %shard_map.41 = (f32[4,256,256]{2,1,0:T(8,128)S(1)}, f32[8,128]{1,0:T(8,128)S(1)}) custom-call(f32[36,256,256]{2,1,0:T(8,128)} %bitcast.6, f32[256,256]{1,0:T(8,128)} %bitcast.7), custom_call_target="tpu_custom_call" | custom-call | tf_op jit(solution)/shard_map/pallas_call | solution.py:620
  52.3 0.6 %slice_bitcast_fusion = f32[40,4]{0,1:T(4,128)} fusion(f32[8,128]{1,0:T(8,128)S(1)} %get-tuple-element.5), kind=kLoop, calls=%fused_computation | loop fusion | bytes 1280 | tf_op jit(solution)/shard_map/transpose | solution.py:656
  52.9 1.0 %copy.5 = f32[4,4,64,256]{3,2,1,0:T(8,128)} copy(f32[4,4,64,256]{3,2,1,0:T(8,128)S(1)} %bitcast.5) | data formatting | bytes 2097152

commit v7 on v6

--- a/solution.py
+++ b/solution.py
@@ -84,8 +84,6 @@
         )
         for p in range(planes)
     ]
-    for copy in last_copies:
-        copy.start()
     all_last = padded.at[0, 2 : planes + 2, 8 : rows_y + 8]
     chunks = rows // CHUNK
 
@@ -93,7 +91,11 @@
         at = pl.ds(pl.multiple_of(c * CHUNK, CHUNK), CHUNK)
         return pltpu.make_async_copy(basis.at[:, at], vecs.at[0:keep, at], load_sem.at[c])
 
-    @pl.loop(0, chunks)
+    load(0).start()
+    for copy in last_copies:
+        copy.start()
+
+    @pl.loop(1, chunks)
     def _(c):
         load(c).start()
 
@@ -327,7 +329,7 @@
     def projected(kind):
         return lane_sum(jnp.sum(proj[kind], axis=1))
 
-    def stencil(step, part):
+    def stencil(step, part, whole=False):
         tall = 16
         lanes = lax.broadcasted_iota(jnp.int32, (tall, width), 1)
         sx, sy, sz = WIND_SPEEDS
@@ -340,9 +342,9 @@
             here = block[8 : tall + 8]
             out_at = pl.ds(pl.multiple_of(p * rows_y + base, 8), tall)
             total = -(react[out_at, :] + centre) * here
-            total = total + padded[step, p + 3, at, :] if p < planes - 1 else total
+            total = total + padded[step, p + 3, at, :] if whole or p < planes - 1 else total
             total = total + (1.0 + 2.0 * sx) * padded[step, p + 1, at, :]
-            total = total - (0.5 * sx) * padded[step, p, at, :] if p > 0 else total
+            total = total - (0.5 * sx) * padded[step, p, at, :] if whole or p > 0 else total
             total = total + roll(block, tall + 15, 0)[8 : tall + 8]
             total = total + (1.0 + 2.0 * sy) * roll(block, 1, 0)[8 : tall + 8]
             total = total - (0.5 * sy) * roll(block, 2, 0)[8 : tall + 8]
@@ -516,6 +518,23 @@
             at = pl.ds(pl.multiple_of(q * 32, 32), 32)
             w_out[step, at, :] = vecs[keep + step, at, :] * scale_row
 
+    def edges_last(step, count, square, scale):
+        wait_halo(step, (6, 7))
+        stencil(step, range(2, planes))
+        project_image(step, span(2, planes - 3), True, square)
+        project_image(step, span(planes - 1))
+        if step > 1:
+            emit(step - 2, scale)
+        wait_halo(step, (0, 1))
+        stencil(step, range(2))
+        project_image(step, span(0))
+        project_image(step, span(1), False, square)
+        for first, second in zip(order[0] + order[1], order[1] + order[0]):
+            wait_halo(step, (first[4],), even)
+            wait_halo(step, (second[4],), odd)
+            p, halo, factor = (jnp.where(even, a, b) for a, b in zip(first[:3], second[:3]))
+            project_late(step, count, p, halo, factor, first[3])
+
     gap = None
     scales = jnp.ones(shape, jnp.float32)
     scales_row = jnp.ones((1, 128), jnp.float32)
@@ -531,21 +550,12 @@
             project(lambda at: vecs[last, at, :], count, 1, everything, True)
             b_row = to_row(projected(1), eye_high)
         square = step == STEPS - 1
-        wait_halo(step, (6, 7))
-        stencil(step, range(2, planes))
-        project_image(step, span(2, planes - 3), True, square)
-        project_image(step, span(planes - 1))
-        if step > 1:
-            emit(step - 2, scale)
-        wait_halo(step, (0, 1))
-        stencil(step, range(2))
-        project_image(step, span(0))
-        project_image(step, span(1), False, square)
-        for first, second in zip(order[0] + order[1], order[1] + order[0]):
-            wait_halo(step, (first[4],), even)
-            wait_halo(step, (second[4],), odd)
-            p, halo, factor = (jnp.where(even, a, b) for a, b in zip(first[:3], second[:3]))
-            project_late(step, count, p, halo, factor, first[3])
+        if step == 0:
+            wait_halo(step, range(8))
+            stencil(step, range(planes), True)
+            project_image(step, everything, True)
+        else:
+            edges_last(step, count, square, scale)
         row = to_row(projected(0)) + b_row
         begin_sum(step, row)
         drain_halo(step)

time: 54 us -> 53.6 us (level)
  no operation moved by 1% of the time
where the time goes in v7:
time: 53.6 us; the launch traced here: 53.5 us
  Pallas kernels  51.3 us (96%)
  local copies, waits for them, and re-layouts  1.55 us (3%)
  between operations  0.64 us (1%)
    pallas_call x1, Pallas kernels, body(): pl.pallas_call(functools.partial(kernel, keep, planes, rows_y, n_gx, n_gy...  51.3 us

profile of v7, /device:TPU:0, one launch (start us, length us, event | category | flops | bytes accessed | tf_op | source)
XLA Modules:
  0.0 53.5 jit_solution(4594461721509733634)
XLA Ops:
  0.6 51.3 %shard_map.41 = (f32[4,256,256]{2,1,0:T(8,128)S(1)}, f32[8,128]{1,0:T(8,128)S(1)}) custom-call(f32[36,256,256]{2,1,0:T(8,128)} %bitcast.6, f32[256,256]{1,0:T(8,128)} %bitcast.7), custom_call_target="tpu_custom_call" | custom-call | tf_op jit(solution)/shard_map/pallas_call | solution.py:630
  51.9 0.6 %slice_bitcast_fusion = f32[40,4]{0,1:T(4,128)} fusion(f32[8,128]{1,0:T(8,128)S(1)} %get-tuple-element.5), kind=kLoop, calls=%fused_computation | loop fusion | bytes 1280 | tf_op jit(solution)/shard_map/transpose | solution.py:666
  52.5 1.0 %copy.5 = f32[4,4,64,256]{3,2,1,0:T(8,128)} copy(f32[4,4,64,256]{3,2,1,0:T(8,128)S(1)} %bitcast.5) | data formatting | bytes 2097152
